TPU v7x, 256 devices: a whole 4x4x8 slice. The times are simulated.
256 devices in a mesh: tm: 32 (over z, y), space: 8 (over x, core).
Axes of the slice: x: 4, y: 4, z: 8, core: 2. Of those that a mesh axis runs over, the one named last changes fastest.
Arguments:
- start_values: float32 [32, 2, 1024, 1024], P('tm', None, 'space'), may hold values from -6 to 6
- node_values: float32 [32, 2, 2, 1024, 1024], P('tm', None, None, 'space'), may hold values from -6 to 6
Outputs:
- next_start: float32 [32, 2, 1024, 1024], P('tm', None, 'space')
- next_nodes: float32 [32, 2, 2, 1024, 1024], P('tm', None, None, 'space')
All inputs are finite; a program needn't handle non-finite values.
Results may differ from a plain program's by a relative error of at most 0.00002.
Values sent between devices are 32-bit elements; how exact they have to be, the bound alone decides.
A program may use at most 64 MiB of HBM per device.

v0:
```python
import jax
import jax.numpy as jnp
from jax import lax
from jax.sharding import Mesh
from jax.sharding import PartitionSpec as P

KX = 1024
KY = 1024
CX = 256
TM = ("tm_0", "tm_1")


diffusion = 1.5
drift = 0.8
shear = 0.6
first_weights = (5.0 / 24.0, 1.0 / 3.0, -1.0 / 24.0)
second_weights = (-1.0 / 24.0, 1.0 / 3.0, 5.0 / 24.0)
whole_weights = (1.0 / 6.0, 2.0 / 3.0, 1.0 / 6.0)


def with_halo(shard, sides, width):
    for axis, dim in sides:
        peers, length = (lax.axis_size(axis), shard.shape[dim])
        up = [(i, (i + 1) % peers) for i in range(peers - 1)]
        down = [(j, i) for i, j in up]
        last = lax.slice_in_dim(shard, length - width, length, axis=dim)
        first = lax.slice_in_dim(shard, 0, width, axis=dim)
        before = lax.ppermute(last, axis, up)
        after = lax.ppermute(first, axis, down)
        shard = jnp.concatenate([before, shard, after], axis=dim)
    return shard


def filled_with(shard, identity):
    return jax.tree.map(
        lambda a, e: jnp.broadcast_to(jnp.asarray(e, a.dtype), a.shape), shard, identity
    )


def carried_in(shard, axes, combine, identity):
    before = start = filled_with(shard, identity)
    running = shard
    for axis in reversed(axes):
        peers, index = (lax.axis_size(axis), lax.axis_index(axis))
        pieces = jax.tree.map(lambda part: lax.all_gather(part, axis), running)
        inside, running = (start, start)
        for k in range(peers):
            passed = k < index
            running = combine(running, jax.tree.map(lambda part: part[k], pieces))
            inside = jax.tree.map(lambda new, old: jnp.where(passed, new, old), running, inside)
        before = combine(inside, before)
    return before


def from_behind(value, axis, steps):
    count = lax.axis_size(axis)
    first, last = (max(0, -steps), min(count, count - steps))
    return lax.ppermute(value, axis, [(source, source + steps) for source in range(first, last)])


def spectrum(row_index, column_index):
    along = (row_index.astype(jnp.float32) - KX // 2) / (KX // 2)
    across = (column_index.astype(jnp.float32) - KY // 2) / (KY // 2)
    real_rate = -diffusion * (along[:, None] * along[:, None] + across[None, :] * across[None, :])
    imag_rate = -drift * across[None, :] + 0.0 * along[:, None]
    return (real_rate, imag_rate, across)


def multiply(real_rate, imag_rate, field):
    return jnp.stack(
        [
            real_rate * field[..., 0, :, :] - imag_rate * field[..., 1, :, :],
            real_rate * field[..., 1, :, :] + imag_rate * field[..., 0, :, :],
        ],
        axis=-3,
    )


def divide(real_part, imag_part, field):
    modulus = real_part * real_part + imag_part * imag_part
    return jnp.stack(
        [
            (field[..., 0, :, :] * real_part + field[..., 1, :, :] * imag_part) / modulus,
            (field[..., 1, :, :] * real_part - field[..., 0, :, :] * imag_part) / modulus,
        ],
        axis=-3,
    )


def explicit(field, across):
    padded = with_halo(field, (("space", 2),), 1)
    sums = padded[..., 2:, :] + padded[..., :-2, :]
    factor = shear * across
    return jnp.stack([factor * sums[..., 1, :, :], -factor * sums[..., 0, :, :]], axis=-3)


def add_pairs(earlier, later):
    return (earlier[0] + later[0], earlier[1] + later[1])


def raised(base_real, base_imag, exponent, places):
    result_real = jnp.ones_like(base_real)
    result_imag = jnp.zeros_like(base_real)
    power_real = base_real
    power_imag = base_imag
    for digit_place in range(places):
        chosen_bit = exponent >> digit_place & 1 == 1
        next_real = result_real * power_real - result_imag * power_imag
        next_imag = result_real * power_imag + result_imag * power_real
        result_real = jnp.where(chosen_bit, next_real, result_real)
        result_imag = jnp.where(chosen_bit, next_imag, result_imag)
        squared_real = power_real * power_real - power_imag * power_imag
        squared_imag = 2.0 * power_real * power_imag
        power_real = squared_real
        power_imag = squared_imag
    return (result_real, result_imag)


def body(start_values, node_values):
    begin_value = start_values[0]
    old_nodes = node_values[0]
    slab_rows = begin_value.shape[1]
    slab_columns = begin_value.shape[2]
    leader = lax.axis_index(TM) == 0
    rank = lax.axis_index("space")
    row_index = rank * slab_rows + lax.iota(jnp.int32, slab_rows)
    real_rate, imag_rate, across = spectrum(row_index, lax.iota(jnp.int32, slab_columns))
    stacked = jnp.stack([begin_value, old_nodes[0], old_nodes[1]])
    old_coupling = explicit(stacked, across)
    old_slopes = multiply(real_rate, imag_rate, stacked) + old_coupling
    sum_one = (
        first_weights[0] * old_slopes[0]
        + first_weights[1] * old_slopes[1]
        + first_weights[2] * old_slopes[2]
    )
    sum_two = (
        second_weights[0] * old_slopes[0]
        + second_weights[1] * old_slopes[1]
        + second_weights[2] * old_slopes[2]
    )
    half_real = 1.0 - 0.5 * real_rate
    half_imag = -0.5 * imag_rate
    node_one = divide(
        half_real,
        half_imag,
        begin_value - 0.5 * multiply(real_rate, imag_rate, old_nodes[0]) + sum_one,
    )
    one_coupling = explicit(node_one[None], across)[0]
    node_two = divide(
        half_real,
        half_imag,
        node_one
        + 0.5 * (one_coupling - old_coupling[1])
        - 0.5 * multiply(real_rate, imag_rate, old_nodes[1])
        + sum_two,
    )
    two_coupling = explicit(node_two[None], across)[0]
    integral = (
        whole_weights[0] * old_slopes[0]
        + whole_weights[1] * (multiply(real_rate, imag_rate, node_one) + one_coupling)
        + whole_weights[2] * (multiply(real_rate, imag_rate, node_two) + two_coupling)
    )
    low_row = KX // 2 - CX // 2
    low_column = KY // 2 - CX // 2
    row_mask = ((row_index >= low_row) & (row_index < low_row + CX)).astype(jnp.float32)[:, None]

    def restrict(field):
        return field[..., low_column : low_column + CX] * row_mask

    def enlarge(field):
        return jnp.pad(field, ((0, 0), (0, 0), (low_column, slab_columns - low_column - CX)))

    coarse_real = real_rate[:, low_column : low_column + CX]
    coarse_imag = imag_rate[:, low_column : low_column + CX]
    begin_coarse = restrict(begin_value)
    end_coarse = restrict(node_two)
    tau = restrict(integral) - 0.5 * multiply(coarse_real, coarse_imag, begin_coarse + end_coarse)
    offset = 0.5 * multiply(coarse_real, coarse_imag, begin_coarse - end_coarse) + tau
    step_real = 1.0 - coarse_real
    step_imag = -coarse_imag
    places = max(1, (lax.axis_size(TM) - 1).bit_length())
    slot = lax.axis_index(TM)
    ones_field = jnp.stack([jnp.ones_like(coarse_real), jnp.zeros_like(coarse_real)])
    gain = divide(step_real, step_imag, ones_field)
    shift_term = divide(step_real, step_imag, jnp.where(leader, begin_coarse + offset, offset))
    scale_real, scale_imag = raised(step_real, step_imag, slot, places)
    weighted = multiply(scale_real, scale_imag, shift_term)
    zeros = jnp.zeros_like(coarse_real)
    summed = carried_in((weighted[0], weighted[1]), TM, add_pairs, (zeros, zeros))
    back_real, back_imag = raised(gain[0], gain[1], jnp.maximum(slot - 1, 0), places)
    begin_new = jnp.where(
        leader, begin_coarse, multiply(back_real, back_imag, jnp.stack([summed[0], summed[1]]))
    )
    end_new = divide(step_real, step_imag, begin_new + offset)
    delta_begin = begin_new - begin_coarse
    delta_end = end_new - end_coarse
    fixed_one = node_one + enlarge(0.5 * (delta_begin + delta_end))
    fixed_two = node_two + enlarge(delta_end)
    arrived = from_behind(fixed_two, TM, 1)
    next_start = jnp.where(leader, begin_value, arrived)
    next_nodes = jnp.stack([fixed_one, fixed_two])
    return (next_start[None], next_nodes[None])


def solution(mesh):
    split = Mesh(mesh.devices.reshape(8, 4, mesh.shape["space"]), ("tm_0", "tm_1", "space"))
    placed = (P(TM, None, "space", None), P(TM, None, None, "space", None))
    return jax.shard_map(
        body,
        mesh=split,
        in_specs=placed,
        out_specs=(P(TM, None, "space", None), P(TM, None, None, "space", None)),
        check_vma=False,
    )
```

profile of v0, /device:TPU:32, one launch (start us, length us, event | category | flops | bytes accessed | tf_op | source)
XLA Modules:
  0.0 176.5 jit_solution(14676135284013154485)
XLA Ops:
  7.2 1.9 %slice_bitcast_fusion.1 = (f32[1,2,128,1024]{3,2,1,0:T(8,128)S(1)}, f32[1,2,128,1024]{3,2,1,0:T(8,128)S(1)}) fusion(f32[1,2,2,128,1024]{4,3,2,1,0:T(8,128)} %param.3), kind=kLoop, calls=%fused_computation.60 | loop fusion | bytes 4194304 | tf_op jit(solution)/shard_map/slice | solution.py:146
  9.1 1.7 collective-permute-start.1
  10.9 1.3 collective-permute-start
  12.2 0.9 broadcast_add_fusion
  13.1 0.9 add_multiply_fusion.11
  14.0 3.3 %fusion.28 = (f32[1,128,1024]{2,1,0:T(8,128)}, f32[1,128,1024]{2,1,0:T(8,128)}, f32[1,128,1024]{2,1,0:T(8,128)}, f32[1,128,1024]{2,1,0:T(8,128)}) fusion(f32[1,2,2,128,1024]{4,3,2,1,0:T(8,128)} %param.3, f32[128]{0:T(128)S(1)} %get-tuple-element.82, f32[1024]{0:T(1024)S(1)} %get-tuple-element.86, f32[1024]{0:T(1024)S(1)} %get-tuple-element.85, ...), kind=kLoop, calls=%fused_computation.73 | loop fusion | flops 1966080 | bytes 4203520 | tf_op jit(solution)/shard_map/sub | solution.py:72
  17.3 1.0 multiply_multiply_fusion.2
  18.3 1.1 add_select_fusion.5
  19.4 0.9 subtract_select_fusion.1
  20.3 1.2 pad_maximum_fusion.7
  21.6 0.8 multiply_subtract_fusion
  22.4 0.6 slice_multiply_fusion
  23.0 1.0 fusion
  24.0 0.2 copy-done.8
  24.2 0.7 fusion.17
  24.9 0.5 fusion.32
  25.6 4.3 %collective-permute-start.3 = (f32[1,2,1,1024]{3,2,1,0:T(1,128)S(1)}, f32[1,2,1,1024]{3,2,1,0:T(1,128)S(1)}, u32[]{:S(2)}, u32[]{:S(2)}) collective-permute-start(f32[1,2,1,1024]{3,2,1,0:T(1,128)S(1)} %get-tuple-element.74), channel_id=1, source_target_pairs={{0,1},{1,2},{2,3},{3,4},{4,5},{5,6},{6,7},{8,9},{9,10},{10,11},{11... | collective-permute-start | bytes 24584 | tf_op jit(solution)/shard_map/ppermute | solution.py:28
  29.9 1.4 collective-permute-start.2
  31.5 2.8 %collective-permute-done.2 = f32[1,2,1,1024]{3,2,1,0:T(1,128)S(1)} collective-permute-done((f32[1,2,1,1024]{3,2,1,0:T(1,128)S(1)}, f32[1,2,1,1024]{3,2,1,0:T(1,128)S(1)}, u32[]{:S(2)}, u32[]{:S(2)}) %collective-permute-start.2) | collective-permute-done | bytes 8224 | tf_op jit(solution)/shard_map/ppermute | solution.py:29
  34.3 0.2 fusion.15
  34.7 0.9 fusion.13
  35.5 0.5 fusion.34
  36.2 0.3 fusion.33
  36.5 4.3 %collective-permute-start.5 = (f32[1,2,1,1024]{3,2,1,0:T(1,128)S(1)}, f32[1,2,1,1024]{3,2,1,0:T(1,128)S(1)}, u32[]{:S(2)}, u32[]{:S(2)}) collective-permute-start(f32[1,2,1,1024]{3,2,1,0:T(1,128)S(1)} %get-tuple-element.70), channel_id=1, source_target_pairs={{0,1},{1,2},{2,3},{3,4},{4,5},{5,6},{6,7},{8,9},{9,10},{10,11},{11... | collective-permute-start | bytes 24584 | tf_op jit(solution)/shard_map/ppermute | solution.py:28
  40.8 1.3 collective-permute-start.4
  42.2 0.9 multiply_multiply_fusion.6
  43.2 0.7 collective-permute-done.4
  43.9 0.2 fusion.14
  44.4 0.2 add_select_fusion
  44.6 0.6 copy-done.9
  45.4 0.9 multiply_add_fusion.1
  46.3 13.9 %all-gather.1 = f32[512,256]{1,0:T(8,128)S(1)} all-gather(f32[128,256]{1,0:T(8,128)S(1)} %get-tuple-element.9), channel_id=3, replica_groups=mesh['tm_0'=8,'tm_1'=4,'space'=8] {'tm_1'}, dimensions={0}, use_global_device_ids=true | all-gather | bytes 655360 | tf_op jit(solution)/shard_map/all_gather | solution.py:45
  60.2 0.8 copy-done.3
  61.0 0.7 fusion.65
  61.8 1.1 multiply_subtract_fusion.1
  62.9 12.8 %all-gather = f32[512,256]{1,0:T(8,128)S(1)} all-gather(f32[128,256]{1,0:T(8,128)S(1)} %multiply_subtract_fusion.1), channel_id=2, replica_groups=mesh['tm_0'=8,'tm_1'=4,'space'=8] {'tm_1'}, dimensions={0}, use_global_device_ids=true | all-gather | bytes 655360 | tf_op jit(solution)/shard_map/all_gather | solution.py:45
  75.7 0.8 copy-done.4
  76.5 0.7 fusion.69
  77.2 1.1 add_select_fusion.9
  78.3 1.8 subtract_select_fusion.6
  80.0 21.9 %all-gather.7.cloned.1.call-done = f32[8,128,256]{2,1,0:T(8,128)} async-done(((f32[1,128,256]{2,1,0:T(8,128)}), f32[8,128,256]{2,1,0:T(8,128)}) %all-gather.7.cloned.1.call-update) | async-done | bytes 1048592 | tf_op jit(solution)/shard_map/all_gather | solution.py:45
  102.0 38.6 %all-gather.5.cloned.1.call-done = f32[8,128,256]{2,1,0:T(8,128)} async-done(((f32[1,128,256]{2,1,0:T(8,128)}), f32[8,128,256]{2,1,0:T(8,128)}) %all-gather.5.cloned.1.call-update) | async-done | bytes 1048592 | tf_op jit(solution)/shard_map/all_gather | solution.py:45
  140.6 2.4 %subtract_bitcast_fusion = (f32[1,128,256]{2,1,0:T(8,128)S(1)}, f32[128,256]{1,0:T(8,128)S(1)}, f32[128,256]{1,0:T(8,128)S(1)}, f32[128,256]{1,0:T(8,128)S(1)}, f32[128,256]{1,0:T(8,128)S(1)}) fusion(pred[]{:T(512)S(6)} %gt.47, pred[]{:T(512)S(6)} %gt.46, f32[512,256]{1,0:T(8,128)} %copy-done.3, pred[]{:T(512)S(6)} %gt.45, pred[]{:T(512)S(6)} %gt.44, ...), kind=kLoop, calls=%fused_computation.166 | loop fusion | flops 2162688 | bytes 4456462 | tf_op jit(solution)/shard_map/stack | solution.py:70
  143.1 1.0 divide_bitcast_fusion.1
  144.4 3.4 %collective-permute-start.6 = (f32[2,128,1024]{2,1,0:T(8,128)S(1)}, f32[2,128,1024]{2,1,0:T(8,128)S(1)}, u32[]{:S(2)}, u32[]{:S(2)}) collective-permute-start(f32[2,128,1024]{2,1,0:T(8,128)S(1)} %pad_add_fusion), channel_id=1, source_target_pairs={{0,8},{8,16},{16,24},{24,32},{32,40},{40,48},{48,56},{56,64},{64,7... | collective-permute-start | bytes 3145736 | tf_op jit(solution)/shard_map/ppermute | solution.py:58
  148.0 1.5 maximum_bitcast_fusion
  149.6 19.0 %collective-permute-done.6 = f32[2,128,1024]{2,1,0:T(8,128)S(1)} collective-permute-done((f32[2,128,1024]{2,1,0:T(8,128)S(1)}, f32[2,128,1024]{2,1,0:T(8,128)S(1)}, u32[]{:S(2)}, u32[]{:S(2)}) %collective-permute-start.6) | collective-permute-done | bytes 1048608 | tf_op jit(solution)/shard_map/ppermute | solution.py:58
  168.6 1.1 select_bitcast_fusion
  (53 shorter events, 2.1 us)
Async XLA Ops:
  7.2 1.9 %copy-start = (f32[1,2,128,1024]{3,2,1,0:T(8,128)S(1)}, f32[1,2,128,1024]{3,2,1,0:T(8,128)}, u32[]{:S(2)}) copy-start(f32[1,2,128,1024]{3,2,1,0:T(8,128)} %param.2) | copy-start | bytes 3145732
  7.2 94.8 %all-gather.7.cloned.1.call-start = ((), (), s32[]{:S(2)}) async-start(), calls=%async_computation.1 | async-start | bytes 1179648 | tf_op jit(solution)/shard_map/all_gather | solution.py:45
  9.1 11.1 %collective-permute-start.1 = (f32[3,2,1,1024]{3,2,1,0:T(1,128)S(1)}, f32[3,2,1,1024]{3,2,1,0:T(1,128)S(1)}, u32[]{:S(2)}, u32[]{:S(2)}) collective-permute-start(f32[3,2,1,1024]{3,2,1,0:T(1,128)S(1)} %get-tuple-element.46), channel_id=1, source_target_pairs={{0,1},{1,2},{2,3},{3,4},{4,5},{5,6},{6,7},{8,9},{9,10},{10,11},{11... | collective-permute-start | bytes 73736 | tf_op jit(solution)/shard_map/ppermute | solution.py:28
  10.9 9.4 %collective-permute-start = (f32[3,2,1,1024]{3,2,1,0:T(1,128)S(1)}, f32[3,2,1,1024]{3,2,1,0:T(1,128)S(1)}, u32[]{:S(2)}, u32[]{:S(2)}) collective-permute-start(f32[3,2,1,1024]{3,2,1,0:T(1,128)S(1)} %get-tuple-element.45), channel_id=1, source_target_pairs={{1,0},{2,1},{3,2},{4,3},{5,4},{6,5},{7,6},{9,8},{10,9},{11,10},{12... | collective-permute-start | bytes 73736 | tf_op jit(solution)/shard_map/ppermute | solution.py:29
  20.3 1.3 copy-start.1
  20.3 1.3 copy-start.2
  23.0 1.0 copy-start.7
  23.0 1.2 copy-start.8
  25.6 5.9 %collective-permute-start.3 = (f32[1,2,1,1024]{3,2,1,0:T(1,128)S(1)}, f32[1,2,1,1024]{3,2,1,0:T(1,128)S(1)}, u32[]{:S(2)}, u32[]{:S(2)}) collective-permute-start(f32[1,2,1,1024]{3,2,1,0:T(1,128)S(1)} %get-tuple-element.74), channel_id=1, source_target_pairs={{0,1},{1,2},{2,3},{3,4},{4,5},{5,6},{6,7},{8,9},{9,10},{10,11},{11... | collective-permute-start | bytes 24584 | tf_op jit(solution)/shard_map/ppermute | solution.py:28
  29.9 4.8 %copy-start.5 = (f32[1,128,1024]{2,1,0:T(8,128)S(1)}, f32[1,128,1024]{2,1,0:T(8,128)}, u32[]{:S(2)}) copy-start(f32[1,128,1024]{2,1,0:T(8,128)} %get-tuple-element.49) | copy-start | bytes 1572868
  29.9 4.8 %copy-start.6 = (f32[1,128,1024]{2,1,0:T(8,128)S(1)}, f32[1,128,1024]{2,1,0:T(8,128)}, u32[]{:S(2)}) copy-start(f32[1,128,1024]{2,1,0:T(8,128)} %get-tuple-element.50) | copy-start | bytes 1572868
  29.9 4.4 %collective-permute-start.2 = (f32[1,2,1,1024]{3,2,1,0:T(1,128)S(1)}, f32[1,2,1,1024]{3,2,1,0:T(1,128)S(1)}, u32[]{:S(2)}, u32[]{:S(2)}) collective-permute-start(f32[1,2,1,1024]{3,2,1,0:T(1,128)S(1)} %get-tuple-element.73), channel_id=1, source_target_pairs={{1,0},{2,1},{3,2},{4,3},{5,4},{6,5},{7,6},{9,8},{10,9},{11,10},{12... | collective-permute-start | bytes 24584 | tf_op jit(solution)/shard_map/ppermute | solution.py:29
  36.5 6.7 %collective-permute-start.5 = (f32[1,2,1,1024]{3,2,1,0:T(1,128)S(1)}, f32[1,2,1,1024]{3,2,1,0:T(1,128)S(1)}, u32[]{:S(2)}, u32[]{:S(2)}) collective-permute-start(f32[1,2,1,1024]{3,2,1,0:T(1,128)S(1)} %get-tuple-element.70), channel_id=1, source_target_pairs={{0,1},{1,2},{2,3},{3,4},{4,5},{5,6},{6,7},{8,9},{9,10},{10,11},{11... | collective-permute-start | bytes 24584 | tf_op jit(solution)/shard_map/ppermute | solution.py:28
  40.8 3.1 %collective-permute-start.4 = (f32[1,2,1,1024]{3,2,1,0:T(1,128)S(1)}, f32[1,2,1,1024]{3,2,1,0:T(1,128)S(1)}, u32[]{:S(2)}, u32[]{:S(2)}) collective-permute-start(f32[1,2,1,1024]{3,2,1,0:T(1,128)S(1)} %get-tuple-element.69), channel_id=1, source_target_pairs={{1,0},{2,1},{3,2},{4,3},{5,4},{6,5},{7,6},{9,8},{10,9},{11,10},{12... | collective-permute-start | bytes 24584 | tf_op jit(solution)/shard_map/ppermute | solution.py:29
  44.2 0.9 copy-start.9
  44.2 1.0 copy-start.10
  44.3 1.0 copy-start.11
  44.3 1.1 copy-start.12
  44.3 1.1 copy-start.13
  60.2 0.8 copy-start.3
  61.7 78.9 %all-gather.5.cloned.1.call-start = ((), (), s32[]{:S(2)}) async-start(), calls=%async_computation | async-start | bytes 1179648 | tf_op jit(solution)/shard_map/all_gather | solution.py:45
  75.7 0.8 copy-start.4
  144.4 24.2 %collective-permute-start.6 = (f32[2,128,1024]{2,1,0:T(8,128)S(1)}, f32[2,128,1024]{2,1,0:T(8,128)S(1)}, u32[]{:S(2)}, u32[]{:S(2)}) collective-permute-start(f32[2,128,1024]{2,1,0:T(8,128)S(1)} %pad_add_fusion), channel_id=1, source_target_pairs={{0,8},{8,16},{16,24},{24,32},{32,40},{40,48},{48,56},{56,64},{64,7... | collective-permute-start | bytes 3145736 | tf_op jit(solution)/shard_map/ppermute | solution.py:58
Sparse Core Ops, SparseCore 0:
  61.8 40.0 all-gather.6
  103.7 36.7 all-gather.4
where the time goes:
time: 177 us
  waiting for transfers between devices  83.1 us (47%)
  other arithmetic  29.8 us (17%)
  blocking collectives  26.7 us (15%)
  starting transfers between devices  17.8 us (10%)
  between operations  14.6 us (8%)
  local copies, waits for them, and re-layouts  4.57 us (3%)
    all_gather x2, waiting for transfers between devices, carried_in(): pieces = jax.tree.map(lambda part: lax.all_gather(part, axis), running)  60.6 us
    all_gather x2, blocking collectives, carried_in(): pieces = jax.tree.map(lambda part: lax.all_gather(part, axis), running)  26.7 us
    ppermute x1, waiting for transfers between devices, from_behind(): lax.ppermute(value, axis, [(source, source + steps) for source in range(f...  19 us
    ppermute x3, starting transfers between devices, with_halo(): before = lax.ppermute(last, axis, up)  10.4 us
    sub x5, other arithmetic, multiply(): real_rate * field[..., 0, :, :] - imag_rate * field[..., 1, :, :]  6.3 us
    ppermute x3, starting transfers between devices, with_halo(): after = lax.ppermute(first, axis, down)  4.01 us
    ppermute x3, waiting for transfers between devices, with_halo(): after = lax.ppermute(first, axis, down)  3.54 us
  transfers between devices with their start and end apart: 9, of which 5 were waited for; matrix products, arithmetic and copies ran while one was open for 9% of the time, Pallas kernels for 0%

commit v1 on v0

v1 whole, which is shorter than its diff:
```python
import functools

import jax
import jax.numpy as jnp
from jax import lax
from jax.experimental import pallas as pl
from jax.experimental.pallas import tpu as pltpu
from jax.sharding import PartitionSpec as P

MESH = pl.DeviceIdType.MESH
F32 = jnp.float32
KX = 1024
KY = 1024
CX = 256
LANES = 128
ROWS = 128
TILES = KY // LANES
FIRST_COARSE_TILE = (KY // 2 - CX // 2) // LANES
COARSE_TILES = CX // LANES
FIRST_COARSE_RANK = (KX // 2 - CX // 2) // ROWS
COARSE_RANKS = CX // ROWS
FINE_TILES = [t for t in range(TILES) if not FIRST_COARSE_TILE <= t < FIRST_COARSE_TILE + COARSE_TILES]

diffusion = 1.5
drift = 0.8
shear = 0.6


def columns(tile):
    return pl.ds(pl.multiple_of(tile * LANES, LANES), LANES)


def rate_of(first_row, first_column, rows):
    row = (first_row + lax.broadcasted_iota(jnp.int32, (rows, LANES), 0)).astype(F32)
    column = (first_column + lax.broadcasted_iota(jnp.int32, (rows, LANES), 1)).astype(F32)
    along = (row - KX // 2) / (KX // 2)
    across = (column - KY // 2) / (KY // 2)
    return -diffusion * (along * along + across * across), -drift * across, shear * across


def times(ar, ai, br, bi):
    return ar * br - ai * bi, ar * bi + ai * br


def inverse(real_part, imag_part):
    scale = 1.0 / (real_part * real_part + imag_part * imag_part)
    return real_part * scale, -imag_part * scale


def kernel(tm_size, space_size, start_hbm, nodes_hbm, next_out, nodes_out, fields, mixed, staged, node_one_buf, whole, offset,
           gathered, scanned, begins, load_sem, halo_send, halo_recv, bulk_send, bulk_recv, gather_send, gather_recv,
           scatter_send, scatter_recv):
    slot = lax.axis_index("tm")
    rank = lax.axis_index("space")
    coarse = (rank >= FIRST_COARSE_RANK) & (rank < FIRST_COARSE_RANK + COARSE_RANKS)
    after = lax.rem(slot + 1, tm_size)
    before = lax.rem(slot + tm_size - 1, tm_size)

    def loads(tile):
        body = pl.ds(8, ROWS)
        return (
            pltpu.make_async_copy(start_hbm.at[:, :, columns(tile)], fields.at[tile, pl.ds(0, 2), body, :], load_sem.at[tile, 0]),
            pltpu.make_async_copy(nodes_hbm.at[:, :, columns(tile)], fields.at[tile, pl.ds(2, 4), body, :], load_sem.at[tile, 1]),
        )

    for tile in range(TILES):
        for copy in loads(tile):
            copy.start()

    barrier = pltpu.get_barrier_semaphore()

    @pl.when(rank > 0)
    def _():
        pl.semaphore_signal(barrier, inc=1, device_id={"tm": slot, "space": rank - 1}, device_id_type=MESH)

    @pl.when(rank < space_size - 1)
    def _():
        pl.semaphore_signal(barrier, inc=1, device_id={"tm": slot, "space": rank + 1}, device_id_type=MESH)

    @pl.when(jnp.logical_not(coarse))
    def _():
        pl.semaphore_signal(barrier, inc=1, device_id={"tm": before, "space": rank}, device_id_type=MESH)

    @pl.when(coarse)
    def _():
        def greet(step, carry):
            pl.semaphore_signal(barrier, inc=1, device_id={"tm": lax.rem(slot + step, tm_size), "space": rank}, device_id_type=MESH)
            return carry

        lax.fori_loop(1, tm_size, greet, 0)

    mixed[:, :, pl.ds(8, 8), :] = jnp.zeros((TILES, 2, 8, LANES), F32)
    mixed[:, :, pl.ds(144, 8), :] = jnp.zeros((TILES, 2, 8, LANES), F32)

    for tile in range(TILES):
        for copy in loads(tile):
            copy.wait()

    @pl.when((rank == 0) | (rank == space_size - 1))
    def _():
        pl.semaphore_wait(barrier, 2)

    @pl.when((rank > 0) & (rank < space_size - 1) & jnp.logical_not(coarse))
    def _():
        pl.semaphore_wait(barrier, 3)

    @pl.when(coarse)
    def _():
        pl.semaphore_wait(barrier, tm_size + 1)

    def halo(side):
        low, high = (ROWS, 0) if side == 0 else (8, ROWS + 8)
        return pltpu.make_async_remote_copy(
            src_ref=fields.at[:, :, pl.ds(low, 8), :], dst_ref=fields.at[:, :, pl.ds(high, 8), :],
            send_sem=halo_send.at[side], recv_sem=halo_recv.at[side],
            device_id={"tm": slot, "space": rank + 1 if side == 0 else rank - 1}, device_id_type=MESH)

    @pl.when(rank < space_size - 1)
    def _():
        halo(0).start()

    @pl.when(rank > 0)
    def _():
        halo(1).start()

    def bulk(rows, cols):
        return pltpu.make_async_remote_copy(
            src_ref=nodes_out.at[pl.ds(2, 2), rows, cols], dst_ref=next_out.at[:, rows, cols],
            send_sem=bulk_send, recv_sem=bulk_recv,
            device_id={"tm": after, "space": rank}, device_id_type=MESH)

    def field(tile, plane, low, high):
        return fields[tile, plane, pl.ds(low + 8, high - low), :]

    def mix(tile, low, high):
        for part in range(2):
            mixed[tile, part, pl.ds(low + 16, high - low), :] = (
                (5.0 / 24.0) * field(tile, part, low, high) + (1.0 / 3.0) * field(tile, 2 + part, low, high)
                - (1.0 / 24.0) * field(tile, 4 + part, low, high))

    def beside(ref, lead, low, high):
        count = high - low
        real = ref[(*lead, 0, pl.ds(low + 15, count), slice(None))] + ref[(*lead, 0, pl.ds(low + 17, count), slice(None))]
        imag = ref[(*lead, 1, pl.ds(low + 15, count), slice(None))] + ref[(*lead, 1, pl.ds(low + 17, count), slice(None))]
        return real, imag

    def rates(tile, low, high):
        return rate_of(rank * ROWS + low, tile * LANES, high - low)

    def one(tile, low, high, scale=None, keep=False):
        rate_real, rate_imag, factor = rates(tile, low, high)
        inv_real, inv_imag = inverse(1.0 - 0.5 * rate_real, -0.5 * rate_imag)
        sum_real, sum_imag = beside(mixed, (tile,), low, high)
        begin = [field(tile, part, low, high) for part in range(2)]
        old_one = [field(tile, 2 + part, low, high) for part in range(2)]
        old_two = [field(tile, 4 + part, low, high) for part in range(2)]
        own = [(5.0 / 24.0) * begin[i] - (1.0 / 6.0) * old_one[i] - (1.0 / 24.0) * old_two[i] for i in range(2)]
        top = times(rate_real, rate_imag, *own)
        node = times(inv_real, inv_imag, begin[0] + top[0] + factor * sum_imag, begin[1] + top[1] - factor * sum_real)
        if scale is not None:
            node = [part * scale for part in node]
        for i in range(2):
            staged[tile, i, pl.ds(low + 16, high - low), :] = (
                (5.0 / 24.0) * old_two[i] - (1.0 / 24.0) * begin[i] - (1.0 / 6.0) * old_one[i] + 0.5 * node[i])
            if keep:
                node_one_buf[i, pl.ds(low + 16, high - low), :] = node[i]
            first, last = max(low, 0), min(high, ROWS)
            if first < last:
                nodes_out[i, pl.ds(first, last - first), columns(tile)] = node[i][first - low:last - low]

    def two(tile, low, high, keep=False):
        rate_real, rate_imag, factor = rates(tile, low, high)
        inv_real, inv_imag = inverse(1.0 - 0.5 * rate_real, -0.5 * rate_imag)
        sum_real, sum_imag = beside(staged, (tile,), low, high)
        begin = [field(tile, part, low, high) for part in range(2)]
        old_one = [field(tile, 2 + part, low, high) for part in range(2)]
        old_two = [field(tile, 4 + part, low, high) for part in range(2)]
        if keep:
            node = [node_one_buf[i, pl.ds(low + 16, high - low), :] for i in range(2)]
        else:
            node = [nodes_out[i, pl.ds(low, high - low), columns(tile)] for i in range(2)]
        own = [(1.0 / 3.0) * old_one[i] - (1.0 / 24.0) * begin[i] - (7.0 / 24.0) * old_two[i] for i in range(2)]
        top = times(rate_real, rate_imag, *own)
        last_node = times(inv_real, inv_imag, node[0] + top[0] + factor * sum_imag, node[1] + top[1] - factor * sum_real)
        for i in range(2):
            if keep:
                whole[i, pl.ds(low + 16, high - low), :] = (
                    (1.0 / 6.0) * begin[i] + (2.0 / 3.0) * node[i] + (1.0 / 6.0) * last_node[i])
            first, last = max(low, 0), min(high, ROWS)
            if first < last:
                nodes_out[2 + i, pl.ds(first, last - first), columns(tile)] = last_node[i][first - low:last - low]

    def inner(tile):
        for low in range(0, ROWS, 32):
            mix(tile, low, low + 32)
        for low in range(0, ROWS, 32):
            one(tile, low, low + 32)
        for low in (8, 40, 72, 104):
            two(tile, low, min(low + 32, 120))

    def rim(tile):
        mix(tile, -8, 0)
        mix(tile, ROWS, ROWS + 8)
        one(tile, -8, 8, scale=jnp.concatenate([jnp.full((8, LANES), (rank > 0).astype(F32)), jnp.ones((8, LANES), F32)]))
        one(tile, 120, 136,
            scale=jnp.concatenate([jnp.ones((8, LANES), F32), jnp.full((8, LANES), (rank < space_size - 1).astype(F32))]))
        two(tile, 0, 8)
        two(tile, 120, 128)

    def wait_halo():
        @pl.when(rank > 0)
        def _():
            halo(0).wait_recv()

        @pl.when(rank < space_size - 1)
        def _():
            halo(1).wait_recv()

        @pl.when(rank == 0)
        def _():
            fields[:, :, pl.ds(0, 8), :] = jnp.zeros((TILES, 6, 8, LANES), F32)

        @pl.when(rank == space_size - 1)
        def _():
            fields[:, :, pl.ds(ROWS + 8, 8), :] = jnp.zeros((TILES, 6, 8, LANES), F32)

    middle = pl.ds(8, 112)
    upper = pl.ds(0, 8)
    lower = pl.ds(120, 8)

    @pl.when(jnp.logical_not(coarse))
    def _():
        def step(tile, carry):
            inner(tile)
            bulk(middle, columns(tile)).start()
            return carry

        lax.fori_loop(0, TILES, step, 0)
        wait_halo()

        def edge(tile, carry):
            rim(tile)
            return carry

        lax.fori_loop(0, TILES, edge, 0)
        bulk(upper, slice(None)).start()
        bulk(lower, slice(None)).start()
        bulk(slice(None), slice(None)).wait()

    @pl.when(coarse)
    def _():
        lead = (slot == 0).astype(F32)
        group, side = slot // COARSE_TILES, lax.rem(slot, COARSE_TILES)

        def piece(index):
            return lax.rem(index, COARSE_TILES), slice(None), pl.ds(pl.multiple_of((index // COARSE_TILES) * 8, 8), 8), slice(None)

        inner(0)
        bulk(middle, columns(0)).start()
        wait_halo()

        def full(tile, carry):
            for low, high in ((-8, 24), (24, 56), (56, 88), (88, 120), (120, 136)):
                mix(tile, low, high)
            for low, high in ((-8, 24), (24, 56), (56, 88), (88, 120), (120, 136)):
                one(tile, low, high, keep=True)
            for low, high in ((-8, 24), (24, 56), (56, 88), (88, 120), (120, 136)):
                two(tile, low, high, keep=True)
            for low in range(0, ROWS, 32):
                rate_real, rate_imag, factor = rates(tile, low, low + 32)
                sum_real, sum_imag = beside(whole, (), low, low + 32)
                own = [whole[i, pl.ds(low + 16, 32), :] - nodes_out[2 + i, pl.ds(low, 32), columns(tile)] for i in range(2)]
                top = times(rate_real, rate_imag, *own)
                offset[tile - FIRST_COARSE_TILE, 0, pl.ds(low, 32), :] = top[0] + factor * sum_imag + lead * field(tile, 0, low, low + 32)
                offset[tile - FIRST_COARSE_TILE, 1, pl.ds(low, 32), :] = top[1] - factor * sum_real + lead * field(tile, 1, low, low + 32)
            return carry

        lax.fori_loop(FIRST_COARSE_TILE, FIRST_COARSE_TILE + COARSE_TILES, full, 0)

        def spread(step, carry):
            peer = lax.rem(slot + step, tm_size)
            pltpu.make_async_remote_copy(
                src_ref=offset.at[piece(peer)], dst_ref=gathered.at[slot], send_sem=gather_send, recv_sem=gather_recv,
                device_id={"tm": peer, "space": rank}, device_id_type=MESH).start()
            return carry

        lax.fori_loop(1, tm_size, spread, 0)
        gathered[slot] = offset[piece(slot)]

        def fine_tile(index):
            return jnp.where(index < FIRST_COARSE_TILE, index, index + COARSE_TILES)

        def step(index, carry):
            tile = fine_tile(index)
            inner(tile)
            bulk(middle, columns(tile)).start()
            return carry

        lax.fori_loop(1, 3, step, 0)

        some = pl.ds(0, tm_size - 1)

        def peers(source, target, send, recv):
            return pltpu.make_async_remote_copy(
                src_ref=source, dst_ref=target, send_sem=send, recv_sem=recv,
                device_id={"tm": after, "space": rank}, device_id_type=MESH)

        arrival = peers(gathered.at[some], gathered.at[some], gather_send, gather_recv)
        arrival.wait_recv()
        rate_real, rate_imag, _ = rate_of(rank * ROWS + group * 8, (FIRST_COARSE_TILE + side) * LANES, 8)
        gain = inverse(1.0 - rate_real, -rate_imag)

        def scan(index, running):
            scanned[index, 0] = running[0]
            scanned[index, 1] = running[1]
            return times(*gain, running[0] + gathered[index, 0], running[1] + gathered[index, 1])

        nothing = jnp.zeros((8, LANES), F32)
        lax.fori_loop(0, tm_size, scan, (nothing, nothing))

        def give(step, carry):
            peer = lax.rem(slot + step, tm_size)
            pltpu.make_async_remote_copy(
                src_ref=scanned.at[peer], dst_ref=begins.at[piece(slot)], send_sem=scatter_send, recv_sem=scatter_recv,
                device_id={"tm": peer, "space": rank}, device_id_type=MESH).start()
            return carry

        lax.fori_loop(1, tm_size, give, 0)
        begins[piece(slot)] = scanned[slot]
        lax.fori_loop(3, len(FINE_TILES), step, 0)

        def edge(index, carry):
            rim(fine_tile(index))
            return carry

        lax.fori_loop(0, len(FINE_TILES), edge, 0)
        left = pl.ds(0, FIRST_COARSE_TILE * LANES)
        right_start = (FIRST_COARSE_TILE + COARSE_TILES) * LANES
        right = pl.ds(right_start, KY - right_start)
        for rows in (upper, lower):
            bulk(rows, left).start()
            bulk(rows, right).start()

        back = peers(scanned.at[some], scanned.at[some], scatter_send, scatter_recv)
        back.wait_recv()
        later = 1.0 - lead

        def finish(tile, carry):
            which = tile - FIRST_COARSE_TILE
            for low in range(0, ROWS, 32):
                rows = pl.ds(low, 32)
                rate_real, rate_imag, _ = rates(tile, low, low + 32)
                inv_real, inv_imag = inverse(1.0 - rate_real, -rate_imag)
                begin_new = [begins[which, i, rows, :] for i in range(2)]
                end_new = times(inv_real, inv_imag, *[begin_new[i] + offset[which, i, rows, :] for i in range(2)])
                for i in range(2):
                    old_end = nodes_out[2 + i, rows, columns(tile)]
                    nodes_out[i, rows, columns(tile)] += 0.5 * (
                        (begin_new[i] - later * field(tile, i, low, low + 32)) + (end_new[i] - old_end))
                    nodes_out[2 + i, rows, columns(tile)] = end_new[i]
                    next_out[i, rows, columns(tile)] = begin_new[i]
            return carry

        lax.fori_loop(FIRST_COARSE_TILE, FIRST_COARSE_TILE + COARSE_TILES, finish, 0)
        arrival.wait_send()
        back.wait_send()
        sent = pl.ds(0, len(FINE_TILES) * LANES)
        bulk(slice(None), sent).wait()

    @pl.when(rank < space_size - 1)
    def _():
        halo(0).wait_send()

    @pl.when(rank > 0)
    def _():
        halo(1).wait_send()

    @pl.when(slot == 0)
    def _():
        def restore(tile, carry):
            for i in range(2):
                next_out[i, :, columns(tile)] = fields[tile, i, pl.ds(8, ROWS), :]
            return carry

        lax.fori_loop(0, TILES, restore, 0)


def solution(mesh):
    tm_size, space_size = mesh.shape["tm"], mesh.shape["space"]

    def body(start_values, node_values):
        any_space = pl.BlockSpec(memory_space=pltpu.MemorySpace.HBM)
        vmem = pl.BlockSpec(memory_space=pltpu.MemorySpace.VMEM)
        dma = pltpu.SemaphoreType.DMA
        next_start, nodes = pl.pallas_call(
            functools.partial(kernel, tm_size, space_size),
            out_shape=(pltpu.MemorySpace.VMEM((2, ROWS, KY), F32), pltpu.MemorySpace.VMEM((4, ROWS, KY), F32)),
            in_specs=[any_space, any_space],
            out_specs=(vmem, vmem),
            scratch_shapes=[
                pltpu.VMEM((TILES, 6, ROWS + 16, LANES), F32),
                pltpu.VMEM((TILES, 2, ROWS + 32, LANES), F32),
                pltpu.VMEM((TILES, 2, ROWS + 32, LANES), F32),
                pltpu.VMEM((2, ROWS + 32, LANES), F32),
                pltpu.VMEM((2, ROWS + 32, LANES), F32),
                pltpu.VMEM((COARSE_TILES, 2, ROWS, LANES), F32),
                pltpu.VMEM((tm_size, 2, 8, LANES), F32),
                pltpu.VMEM((tm_size, 2, 8, LANES), F32),
                pltpu.VMEM((COARSE_TILES, 2, ROWS, LANES), F32),
                dma((TILES, 2)),
                dma((2,)),
                dma((2,)),
                dma,
                dma,
                dma,
                dma,
                dma,
                dma,
            ],
            compiler_params=pltpu.CompilerParams(collective_id=0, has_side_effects=True, vmem_limit_bytes=61696 * 1024),
            name="pfasst",
        )(start_values[0], node_values[0].reshape(4, ROWS, KY))
        return next_start[None], nodes.reshape(1, 2, 2, ROWS, KY)

    return jax.shard_map(
        body,
        mesh=mesh,
        in_specs=(P("tm", None, "space", None), P("tm", None, None, "space", None)),
        out_specs=(P("tm", None, "space", None), P("tm", None, None, "space", None)),
        check_vma=False,
    )
```

time: 177 us -> 40.5 us (0.23)
  the two profiles are of different devices: /device:TPU:32 before, /device:TPU:3 now
where the time goes in v1:
time: 40.5 us; the launch traced here: 40.4 us
  Pallas kernels  37.4 us (92%)
  local copies, waits for them, and re-layouts  2.29 us (6%)
  between operations  0.64 us (2%)
    pallas_call x1, Pallas kernels, body(): pl.pallas_call(functools.partial(kernel, tm_size, space_size), out_shape=...  37.4 us
    unnamed x2, local copies, waits for them, and re-layouts  2.29 us

profile of v1, /device:TPU:3, one launch (start us, length us, event | category | flops | bytes accessed | tf_op | source)
XLA Modules:
  0.0 40.4 jit_solution(7298851798369675121)
XLA Ops:
  0.6 37.4 %pfasst.1 = (f32[2,128,1024]{2,1,0:T(8,128)S(1)}, f32[4,128,1024]{2,1,0:T(8,128)S(1)}) custom-call(f32[2,128,1024]{2,1,0:T(8,128)} %bitcast.7, f32[4,128,1024]{2,1,0:T(8,128)} %bitcast.6), custom_call_target="tpu_custom_call" | custom-call | tf_op jit(solution)/shard_map/pfasst/pallas_call | solution.py:395
  38.1 1.0 %copy.6 = f32[1,2,128,1024]{3,2,1,0:T(8,128)} copy(f32[1,2,128,1024]{3,2,1,0:T(8,128)S(1)} %bitcast.5) | data formatting | bytes 2097152
  39.0 1.3 %copy.7 = f32[1,2,2,128,1024]{4,3,2,1,0:T(8,128)} copy(f32[1,2,2,128,1024]{4,3,2,1,0:T(8,128)S(1)} %bitcast.4) | data formatting | bytes 4194304

commit v2 on v1

v2 whole, which is shorter than its diff:
```python
import functools

import jax
import jax.numpy as jnp
from jax import lax
from jax.experimental import pallas as pl
from jax.experimental.pallas import tpu as pltpu
from jax.sharding import PartitionSpec as P

MESH = pl.DeviceIdType.MESH
F32 = jnp.float32
KX = 1024
KY = 1024
CX = 256
LANES = 128
ROWS = 128
TILES = KY // LANES
FIRST_COARSE_TILE = (KY // 2 - CX // 2) // LANES
COARSE_TILES = CX // LANES
FIRST_COARSE_RANK = (KX // 2 - CX // 2) // ROWS
COARSE_RANKS = CX // ROWS
FINE_TILES = TILES - COARSE_TILES
RING = 4
GROUP = 16
PIECE_ROWS = COARSE_TILES * ROWS // GROUP
RELAY_SHARED = 1
RELAY_WRAP = 0
RELAYS = 2 * (2 + RELAY_SHARED + RELAY_WRAP)
RELAY_ROWS = 56
EARLY = 5
EARLY_WRAP = 5

diffusion = 1.5
drift = 0.8
shear = 0.6


def columns(tile):
    return pl.ds(pl.multiple_of(tile * LANES, LANES), LANES)


def rate_of(first_row, first_column, rows):
    row = (first_row + lax.broadcasted_iota(jnp.int32, (rows, LANES), 0)).astype(F32)
    column = (first_column + lax.broadcasted_iota(jnp.int32, (rows, LANES), 1)).astype(F32)
    along = (row - KX // 2) / (KX // 2)
    across = (column - KY // 2) / (KY // 2)
    return -diffusion * (along * along + across * across), -drift * across, shear * across


def times(ar, ai, br, bi):
    return ar * br - ai * bi, ar * bi + ai * br


def inverse(real_part, imag_part):
    scale = 1.0 / (real_part * real_part + imag_part * imag_part)
    return real_part * scale, -imag_part * scale


def tile_at(index):
    early = jnp.where(index < COARSE_TILES, index + FIRST_COARSE_TILE, index - COARSE_TILES)
    return jnp.where(index < FIRST_COARSE_TILE + COARSE_TILES, early, index)


def kernel(tm_size, space_size, start_hbm, nodes_hbm, next_out, nodes_out, fields, mixed, staged, node_one_buf, whole, offset,
           gathered, carry_in, carry_out, results, begins, first_leg, second_leg, load_sem, halo_send, halo_recv, bulk_send,
           bulk_recv, gather_send, gather_recv, carry_send, carry_recv, scatter_send, scatter_recv, relay_send, relay_recv,
           ready, ready_carry, aside, aside_send, aside_recv):
    slot = lax.axis_index("tm")
    rank = lax.axis_index("space")
    coarse = (rank >= FIRST_COARSE_RANK) & (rank < FIRST_COARSE_RANK + COARSE_RANKS)
    fine = jnp.logical_not(coarse)
    shared = (rank == FIRST_COARSE_RANK - 1) | (rank == FIRST_COARSE_RANK + COARSE_RANKS)
    column, place = slot // RING, lax.rem(slot, RING)

    def at_slot(index):
        return {"tm": lax.rem(index, tm_size), "space": rank}

    after = slot + 1
    before = slot + tm_size - 1
    above = column * RING + lax.rem(place + 1, RING)
    below = column * RING + lax.rem(place + RING - 1, RING)

    def loads(tile):
        body = pl.ds(8, ROWS)
        return (
            pltpu.make_async_copy(start_hbm.at[:, :, columns(tile)], fields.at[tile, pl.ds(0, 2), body, :], load_sem.at[tile, 0]),
            pltpu.make_async_copy(nodes_hbm.at[:, :, columns(tile)], fields.at[tile, pl.ds(2, 4), body, :], load_sem.at[tile, 1]),
        )

    def wait_load(tile):
        for copy in loads(tile):
            copy.wait()

    barrier = pltpu.get_barrier_semaphore()

    def greet(target):
        pl.semaphore_signal(barrier, inc=1, device_id=target, device_id_type=MESH)

    @pl.when(rank > 0)
    def _():
        greet({"tm": slot, "space": rank - 1})

    @pl.when(rank < space_size - 1)
    def _():
        greet({"tm": slot, "space": rank + 1})

    greet(at_slot(before))

    @pl.when(fine)
    def _():
        greet(at_slot(above))

        @pl.when(place == 0)
        def _():
            greet(at_slot(slot + tm_size - RING + 1))

    member, group = lax.rem(slot, GROUP), slot // GROUP
    groups = tm_size // GROUP
    depth = GROUP // RING

    def in_group(index):
        return at_slot(group * GROUP + index)

    def facing(step):
        return at_slot((group + step) * GROUP + (depth - 1 - member // RING) * RING + place)

    @pl.when(coarse)
    def _():
        def call(index, carry):
            greet(in_group(index))
            return carry

        lax.fori_loop(member + 1, GROUP, call, 0)

        @pl.when(group < groups - 1)
        def _():
            greet(facing(1))

    def begin_load(index, carry):
        for copy in loads(tile_at(index)):
            copy.start()
        return carry

    lax.fori_loop(0, TILES, begin_load, 0)
    mixed[:, :, pl.ds(8, 8), :] = jnp.zeros((TILES, 2, 8, LANES), F32)
    mixed[:, :, pl.ds(144, 8), :] = jnp.zeros((TILES, 2, 8, LANES), F32)

    with jax.named_scope("load"):
        for tile in range(FIRST_COARSE_TILE, FIRST_COARSE_TILE + COARSE_TILES):
            wait_load(tile)

    def count(flag):
        return flag.astype(jnp.int32)

    with jax.named_scope("barrier"):
        own_kind = jnp.where(coarse, member + count(group > 0), 1 + count(place == 1))
        pl.semaphore_wait(barrier, 1 + count(rank > 0) + count(rank < space_size - 1) + own_kind)

    @pl.when(coarse)
    def _():
        @pl.when(group > 0)
        def _():
            pl.semaphore_signal(ready_carry, inc=1, device_id=facing(-1), device_id_type=MESH)

        def answer(index, carry):
            pl.semaphore_signal(ready, inc=1, device_id=in_group(index), device_id_type=MESH)
            return carry

        lax.fori_loop(0, member, answer, 0)

    parts = (pl.ds(FIRST_COARSE_TILE, COARSE_TILES), pl.ds(0, FIRST_COARSE_TILE),
             pl.ds(FIRST_COARSE_TILE + COARSE_TILES, TILES - FIRST_COARSE_TILE - COARSE_TILES))

    def halo(side, part):
        low, high = (ROWS, 0) if side == 0 else (8, ROWS + 8)
        return pltpu.make_async_remote_copy(
            src_ref=fields.at[parts[part], :, pl.ds(low, 8), :], dst_ref=fields.at[parts[part], :, pl.ds(high, 8), :],
            send_sem=halo_send.at[side, part], recv_sem=halo_recv.at[side, part],
            device_id={"tm": slot, "space": rank + 1 if side == 0 else rank - 1}, device_id_type=MESH)

    def send_halo(*which):
        @pl.when(rank < space_size - 1)
        def _():
            for part in which:
                halo(0, part).start()

        @pl.when(rank > 0)
        def _():
            for part in which:
                halo(1, part).start()

    def wait_halo(*which):
        @pl.when(rank > 0)
        def _():
            for part in which:
                halo(0, part).wait_recv()

        @pl.when(rank < space_size - 1)
        def _():
            for part in which:
                halo(1, part).wait_recv()

    send_halo(0)

    def bulk(rows, cols, index=0):
        return pltpu.make_async_remote_copy(
            src_ref=nodes_out.at[pl.ds(2, 2), rows, cols], dst_ref=next_out.at[:, rows, cols],
            send_sem=bulk_send.at[index], recv_sem=bulk_recv, device_id=at_slot(after), device_id_type=MESH)

    def push(rows, cols, index):
        @pl.when(slot < tm_size - 1)
        def _():
            bulk(rows, cols, index).start()

    def field(tile, plane, low, high):
        return fields[tile, plane, pl.ds(low + 8, high - low), :]

    def mix(tile, low, high):
        for part in range(2):
            mixed[tile, part, pl.ds(low + 16, high - low), :] = (
                (5.0 / 24.0) * field(tile, part, low, high) + (1.0 / 3.0) * field(tile, 2 + part, low, high)
                - (1.0 / 24.0) * field(tile, 4 + part, low, high))

    def beside(ref, lead, low, high):
        count = high - low
        real = ref[(*lead, 0, pl.ds(low + 15, count), slice(None))] + ref[(*lead, 0, pl.ds(low + 17, count), slice(None))]
        imag = ref[(*lead, 1, pl.ds(low + 15, count), slice(None))] + ref[(*lead, 1, pl.ds(low + 17, count), slice(None))]
        return real, imag

    def rates(tile, low, high):
        return rate_of(rank * ROWS + low, tile * LANES, high - low)

    def one(tile, low, high, scale=None, keep=False):
        rate_real, rate_imag, factor = rates(tile, low, high)
        inv_real, inv_imag = inverse(1.0 - 0.5 * rate_real, -0.5 * rate_imag)
        sum_real, sum_imag = beside(mixed, (tile,), low, high)
        begin = [field(tile, part, low, high) for part in range(2)]
        old_one = [field(tile, 2 + part, low, high) for part in range(2)]
        old_two = [field(tile, 4 + part, low, high) for part in range(2)]
        own = [(5.0 / 24.0) * begin[i] - (1.0 / 6.0) * old_one[i] - (1.0 / 24.0) * old_two[i] for i in range(2)]
        top = times(rate_real, rate_imag, *own)
        node = times(inv_real, inv_imag, begin[0] + top[0] + factor * sum_imag, begin[1] + top[1] - factor * sum_real)
        if scale is not None:
            node = [part * scale for part in node]
        for i in range(2):
            staged[tile, i, pl.ds(low + 16, high - low), :] = (
                (5.0 / 24.0) * old_two[i] - (1.0 / 24.0) * begin[i] - (1.0 / 6.0) * old_one[i] + 0.5 * node[i])
            if keep:
                node_one_buf[i, pl.ds(low + 16, high - low), :] = node[i]
            first, last = max(low, 0), min(high, ROWS)
            if first < last:
                nodes_out[i, pl.ds(first, last - first), columns(tile)] = node[i][first - low:last - low]

    def two(tile, low, high, keep=False):
        rate_real, rate_imag, factor = rates(tile, low, high)
        inv_real, inv_imag = inverse(1.0 - 0.5 * rate_real, -0.5 * rate_imag)
        sum_real, sum_imag = beside(staged, (tile,), low, high)
        begin = [field(tile, part, low, high) for part in range(2)]
        old_one = [field(tile, 2 + part, low, high) for part in range(2)]
        old_two = [field(tile, 4 + part, low, high) for part in range(2)]
        if keep:
            node = [node_one_buf[i, pl.ds(low + 16, high - low), :] for i in range(2)]
        else:
            node = [nodes_out[i, pl.ds(low, high - low), columns(tile)] for i in range(2)]
        own = [(1.0 / 3.0) * old_one[i] - (1.0 / 24.0) * begin[i] - (7.0 / 24.0) * old_two[i] for i in range(2)]
        top = times(rate_real, rate_imag, *own)
        last_node = times(inv_real, inv_imag, node[0] + top[0] + factor * sum_imag, node[1] + top[1] - factor * sum_real)
        for i in range(2):
            if keep:
                whole[i, pl.ds(low + 16, high - low), :] = (
                    (1.0 / 6.0) * begin[i] + (2.0 / 3.0) * node[i] + (1.0 / 6.0) * last_node[i])
            first, last = max(low, 0), min(high, ROWS)
            if first < last:
                nodes_out[2 + i, pl.ds(first, last - first), columns(tile)] = last_node[i][first - low:last - low]

    def inner(tile):
        for low in range(0, ROWS, 32):
            mix(tile, low, low + 32)
        for low in range(0, ROWS, 32):
            one(tile, low, low + 32)
        for low in (8, 40, 72, 104):
            two(tile, low, min(low + 32, 120))

    def rim(tile):
        mix(tile, -8, 0)
        mix(tile, ROWS, ROWS + 8)
        one(tile, -8, 8, scale=jnp.concatenate([jnp.full((8, LANES), (rank > 0).astype(F32)), jnp.ones((8, LANES), F32)]))
        one(tile, 120, 136,
            scale=jnp.concatenate([jnp.ones((8, LANES), F32), jnp.full((8, LANES), (rank < space_size - 1).astype(F32))]))
        two(tile, 0, 8)
        two(tile, 120, 128)

    middle = pl.ds(8, 112)
    upper = pl.ds(0, 8)
    lower = pl.ds(120, 8)

    def inner_push(index, carry):
        tile = tile_at(index)
        wait_load(tile)
        inner(tile)
        push(middle, columns(tile), index)
        return carry

    def edge(index, carry):
        rim(tile_at(index))
        return carry

    def settle(cols):
        @pl.when(slot > 0)
        def _():
            bulk(slice(None), cols).wait_recv()

    @pl.when(fine)
    def _():
        def relay_source(chunk):
            rows = pl.ds(pl.multiple_of(8 + lax.rem(chunk, 2) * RELAY_ROWS, 8), RELAY_ROWS)
            return rows, columns(tile_at(chunk // 2))

        def leg(which, chunk):
            rows, cols = relay_source(chunk)
            if which == 0:
                source, target, device = nodes_out.at[pl.ds(2, 2), rows, cols], first_leg.at[chunk], at_slot(below)
                recv = relay_recv.at[0, chunk]
            elif which == 1:
                source, target, device, recv = first_leg.at[chunk], second_leg.at[chunk], at_slot(below), relay_recv.at[1, chunk]
            else:
                origin = column * RING + lax.rem(place + 2, RING)
                source, target, device, recv = second_leg.at[chunk], next_out.at[:, rows, cols], at_slot(origin + 1), bulk_recv
            return pltpu.make_async_remote_copy(
                src_ref=source, dst_ref=target, send_sem=relay_send.at[which, chunk], recv_sem=recv,
                device_id=device, device_id_type=MESH)

        def relayed(which):
            start = lax.rem(place + which, RING)
            wraps = (start == RING - 1).astype(jnp.int32)
            return 2 + RELAY_SHARED * shared.astype(jnp.int32) + RELAY_WRAP * wraps

        def has_origin(which):
            return column * RING + lax.rem(place + which, RING) < tm_size - 1

        def start_tile(index, carry):
            @pl.when(index >= COARSE_TILES)
            def _():
                wait_load(tile_at(index))

            inner(tile_at(index))

            @pl.when(has_origin(0) & (index < relayed(0)))
            def _():
                leg(0, 2 * index).start()
                leg(0, 2 * index + 1).start()

            @pl.when(has_origin(0) & (index >= relayed(0)))
            def _():
                bulk(middle, columns(tile_at(index)), index).start()

            return carry

        def forward(which, chunk):
            @pl.when(has_origin(which) & (chunk < 2 * relayed(which)))
            def _():
                leg(which - 1, chunk).wait_recv()
                leg(which, chunk).start()

        with jax.named_scope("inner"):
            lax.fori_loop(0, TILES, start_tile, 0)
        send_halo(1, 2)
        with jax.named_scope("fwdA"):
            forward(1, 0)
            forward(1, 1)
        with jax.named_scope("halo"):
            wait_halo(0, 1, 2)

        @pl.when(rank == 0)
        def _():
            fields[:, :, pl.ds(0, 8), :] = jnp.zeros((TILES, 6, 8, LANES), F32)

        @pl.when(rank == space_size - 1)
        def _():
            fields[:, :, pl.ds(ROWS + 8, 8), :] = jnp.zeros((TILES, 6, 8, LANES), F32)

        with jax.named_scope("rim"):
            lax.fori_loop(0, TILES, edge, 0)
        push(upper, slice(None), TILES)
        push(lower, slice(None), TILES + 1)

        def pass_on(step, carry):
            forward(1, step)
            forward(2, step - 2)
            return carry

        with jax.named_scope("fwdB"):
            lax.fori_loop(2, RELAYS + 2, pass_on, 0)
        with jax.named_scope("settle"):
            settle(slice(None))

        @pl.when(slot < tm_size - 1)
        def _():
            def sent(index, carry):
                @pl.when(index >= relayed(0))
                def _():
                    bulk(middle, columns(tile_at(index)), index).wait_send()

                return carry

            lax.fori_loop(0, TILES, sent, 0)
            bulk(upper, slice(None), TILES).wait_send()
            bulk(lower, slice(None), TILES + 1).wait_send()

        for which in range(3):
            def legs_sent(chunk, carry):
                @pl.when(has_origin(which) & (chunk < 2 * relayed(which)))
                def _():
                    leg(which, chunk).wait_send()

                return carry

            lax.fori_loop(0, RELAYS, legs_sent, 0)

    @pl.when(coarse)
    def _():
        lead = (slot == 0).astype(F32)

        def piece(index):
            row = index // RING
            number = jnp.where(lax.rem(group, 2) == 1, depth - 1 - row, row) * RING + lax.rem(index, RING)
            share = GROUP // COARSE_TILES
            rows = pl.ds(pl.multiple_of(lax.rem(number, share) * PIECE_ROWS, 8), PIECE_ROWS)
            return number // share, slice(None), rows, slice(None)

        def inner_only(index, carry):
            inner(tile_at(index))
            return carry

        def push_only(index, carry):
            push(middle, columns(tile_at(index)), index)
            return carry

        lax.fori_loop(COARSE_TILES, TILES, lambda index, carry: (wait_load(tile_at(index)), carry)[1], 0)
        send_halo(1, 2)
        with jax.named_scope("innerA"):
            lax.fori_loop(COARSE_TILES, TILES, inner_only, 0)
        with jax.named_scope("halo"):
            wait_halo(0)

        def full(tile, carry):
            bands = ((-8, 24), (24, 56), (56, 88), (88, 120), (120, 136))
            for low, high in bands:
                mix(tile, low, high)
            for low, high in bands:
                one(tile, low, high, keep=True)
            for low, high in bands:
                two(tile, low, high, keep=True)
            for low in range(0, ROWS, 32):
                rate_real, rate_imag, factor = rates(tile, low, low + 32)
                sum_real, sum_imag = beside(whole, (), low, low + 32)
                own = [whole[i, pl.ds(low + 16, 32), :] - nodes_out[2 + i, pl.ds(low, 32), columns(tile)] for i in range(2)]
                top = times(rate_real, rate_imag, *own)
                offset[tile - FIRST_COARSE_TILE, 0, pl.ds(low, 32), :] = top[0] + factor * sum_imag + lead * field(tile, 0, low, low + 32)
                offset[tile - FIRST_COARSE_TILE, 1, pl.ds(low, 32), :] = top[1] - factor * sum_real + lead * field(tile, 1, low, low + 32)
            return carry

        def gather(source, target):
            return pltpu.make_async_remote_copy(
                src_ref=offset.at[piece(target)], dst_ref=gathered.at[source], send_sem=gather_send.at[target],
                recv_sem=gather_recv.at[source], device_id=in_group(target), device_id_type=MESH)

        def scatter(source, target):
            return pltpu.make_async_remote_copy(
                src_ref=results.at[target], dst_ref=begins.at[piece(source)], send_sem=scatter_send.at[target],
                recv_sem=scatter_recv.at[source], device_id=in_group(target), device_id_type=MESH)

        def hand_on():
            return pltpu.make_async_remote_copy(
                src_ref=carry_out, dst_ref=carry_in, send_sem=carry_send, recv_sem=carry_recv, device_id=facing(1),
                device_id_type=MESH)

        row = member // RING
        beside_row = (row + 1 - 2 * lax.rem(row, 2)) * RING

        def detour(stage):
            source = offset.at[piece(row * RING)] if stage == 0 else results.at[row * RING]
            sem = gather_send if stage == 0 else scatter_send
            return pltpu.make_async_remote_copy(
                src_ref=source, dst_ref=aside.at[stage], send_sem=sem.at[row * RING], recv_sem=aside_recv.at[stage],
                device_id=in_group(beside_row), device_id_type=MESH)

        def relay_aside(stage):
            origin = beside_row + RING - 1
            target = gathered.at[origin] if stage == 0 else begins.at[piece(origin)]
            sem = gather_recv if stage == 0 else scatter_recv
            return pltpu.make_async_remote_copy(
                src_ref=aside.at[stage], dst_ref=target, send_sem=aside_send.at[stage], recv_sem=sem.at[origin],
                device_id=in_group(beside_row), device_id_type=MESH)

        def pass_aside(stage):
            @pl.when(place == 0)
            def _():
                detour(stage).wait_recv()
                relay_aside(stage).start()

        def blocked(target):
            return (place == RING - 1) & (target == row * RING)

        def other(distance):
            return lax.rem(member + distance, GROUP)

        with jax.named_scope("full"):
            lax.fori_loop(FIRST_COARSE_TILE, FIRST_COARSE_TILE + COARSE_TILES, full, 0)
        with jax.named_scope("ready"):
            @pl.when(member < GROUP - 1)
            def _():
                pl.semaphore_wait(ready, GROUP - 1 - member)

        def spread(distance, carry):
            @pl.when(jnp.logical_not(blocked(other(distance))))
            def _():
                gather(member, other(distance)).start()

            return carry

        with jax.named_scope("spread"):
            @pl.when(place == RING - 1)
            def _():
                detour(0).start()

            lax.fori_loop(1, GROUP, spread, 0)
        gathered[member] = offset[piece(member)]
        early = jnp.where(place == RING - 1, EARLY_WRAP, EARLY)
        lax.fori_loop(COARSE_TILES, early, push_only, 0)
        tile, _, _, _ = piece(member)
        number = jnp.where(lax.rem(group, 2) == 1, depth - 1 - member // RING, member // RING) * RING + place
        first = lax.rem(number, GROUP // COARSE_TILES) * PIECE_ROWS
        rate_real, rate_imag, _ = rate_of(rank * ROWS + first, (FIRST_COARSE_TILE + tile) * LANES, PIECE_ROWS)
        gain = inverse(1.0 - rate_real, -rate_imag)

        with jax.named_scope("aside0"):
            pass_aside(0)
        with jax.named_scope("gather"):
            def arrive(distance, carry):
                gather(other(distance), member).wait_recv()
                return carry

            lax.fori_loop(1, GROUP, arrive, 0)

        with jax.named_scope("carry"):
            @pl.when(group == 0)
            def _():
                carry_in[...] = jnp.zeros((2, PIECE_ROWS, LANES), F32)

            @pl.when(group > 0)
            def _():
                hand_on().wait_recv()

        def scan(index, running):
            for i in range(2):
                results[index, i] = running[i]
            return times(*gain, running[0] + gathered[index, 0], running[1] + gathered[index, 1])

        with jax.named_scope("scan"):
            running = lax.fori_loop(0, GROUP, scan, (carry_in[0], carry_in[1]))
            for i in range(2):
                carry_out[i] = running[i]

            @pl.when(group < groups - 1)
            def _():
                pl.semaphore_wait(ready_carry, 1)
                hand_on().start()

        def give(distance, carry):
            @pl.when(jnp.logical_not(blocked(other(distance))))
            def _():
                scatter(member, other(distance)).start()

            return carry

        with jax.named_scope("give"):
            @pl.when(place == RING - 1)
            def _():
                detour(1).start()

            lax.fori_loop(1, GROUP, give, 0)
        begins[piece(member)] = results[member]
        lax.fori_loop(early, TILES, push_only, 0)
        with jax.named_scope("halo2"):
            wait_halo(1, 2)
        with jax.named_scope("rim"):
            lax.fori_loop(COARSE_TILES, TILES, edge, 0)
        left = pl.ds(0, FIRST_COARSE_TILE * LANES)
        right_start = (FIRST_COARSE_TILE + COARSE_TILES) * LANES
        right = pl.ds(right_start, KY - right_start)
        rims = [(upper, left), (upper, right), (lower, left), (lower, right)]
        for number, (rows, cols) in enumerate(rims):
            push(rows, cols, TILES + number)

        with jax.named_scope("aside1"):
            pass_aside(1)
        with jax.named_scope("back"):
            def fetch(distance, carry):
                scatter(other(distance), member).wait_recv()
                return carry

            lax.fori_loop(1, GROUP, fetch, 0)

        later = 1.0 - lead

        def finish(tile, carry):
            which = tile - FIRST_COARSE_TILE
            for low in range(0, ROWS, 32):
                rows = pl.ds(low, 32)
                rate_real, rate_imag, _ = rates(tile, low, low + 32)
                inv_real, inv_imag = inverse(1.0 - rate_real, -rate_imag)
                begin_new = [begins[which, i, rows, :] for i in range(2)]
                end_new = times(inv_real, inv_imag, *[begin_new[i] + offset[which, i, rows, :] for i in range(2)])
                for i in range(2):
                    old_end = nodes_out[2 + i, rows, columns(tile)]
                    nodes_out[i, rows, columns(tile)] += 0.5 * (
                        (begin_new[i] - later * field(tile, i, low, low + 32)) + (end_new[i] - old_end))
                    nodes_out[2 + i, rows, columns(tile)] = end_new[i]
                    next_out[i, rows, columns(tile)] = begin_new[i]
            return carry

        with jax.named_scope("finish"):
            lax.fori_loop(FIRST_COARSE_TILE, FIRST_COARSE_TILE + COARSE_TILES, finish, 0)

        with jax.named_scope("settle"):
            settle(pl.ds(0, FINE_TILES * LANES))

        @pl.when(slot < tm_size - 1)
        def _():
            def sent(index, carry):
                bulk(middle, columns(tile_at(index)), index).wait_send()
                return carry

            lax.fori_loop(COARSE_TILES, TILES, sent, 0)
            for number, (rows, cols) in enumerate(rims):
                bulk(rows, cols, TILES + number).wait_send()

        @pl.when(group < groups - 1)
        def _():
            hand_on().wait_send()

        def let_go(distance, carry):
            gather(member, other(distance)).wait_send()
            scatter(member, other(distance)).wait_send()
            return carry

        lax.fori_loop(1, GROUP, let_go, 0)

        @pl.when(place == 0)
        def _():
            for stage in range(2):
                relay_aside(stage).wait_send()

    @pl.when(rank < space_size - 1)
    def _():
        for part in range(3):
            halo(0, part).wait_send()

    @pl.when(rank > 0)
    def _():
        for part in range(3):
            halo(1, part).wait_send()

    @pl.when(slot == 0)
    def _():
        def restore(tile, carry):
            for i in range(2):
                next_out[i, :, columns(tile)] = fields[tile, i, pl.ds(8, ROWS), :]
            return carry

        lax.fori_loop(0, TILES, restore, 0)


def deliver(start_ref, nodes_ref, start_hbm, nodes_hbm, sems):
    copies = [pltpu.make_async_copy(nodes_ref.at[i], nodes_hbm.at[i], sems.at[i]) for i in range(4)]
    copies += [pltpu.make_async_copy(start_ref.at[i], start_hbm.at[i], sems.at[4 + i]) for i in range(2)]
    for copy in copies:
        copy.start()
    for copy in copies:
        copy.wait()


def solution(mesh):
    tm_size, space_size = mesh.shape["tm"], mesh.shape["space"]

    def body(start_values, node_values):
        hbm = pl.BlockSpec(memory_space=pltpu.MemorySpace.HBM)
        vmem = pl.BlockSpec(memory_space=pltpu.MemorySpace.VMEM)
        dma = pltpu.SemaphoreType.DMA
        next_start, nodes = pl.pallas_call(
            functools.partial(kernel, tm_size, space_size),
            out_shape=(pltpu.MemorySpace.VMEM((2, ROWS, KY), F32), pltpu.MemorySpace.VMEM((4, ROWS, KY), F32)),
            in_specs=[hbm, hbm],
            out_specs=(vmem, vmem),
            scratch_shapes=[
                pltpu.VMEM((TILES, 6, ROWS + 16, LANES), F32),
                pltpu.VMEM((TILES, 2, ROWS + 32, LANES), F32),
                pltpu.VMEM((TILES, 2, ROWS + 32, LANES), F32),
                pltpu.VMEM((2, ROWS + 32, LANES), F32),
                pltpu.VMEM((2, ROWS + 32, LANES), F32),
                pltpu.VMEM((COARSE_TILES, 2, ROWS, LANES), F32),
                pltpu.VMEM((GROUP, 2, PIECE_ROWS, LANES), F32),
                pltpu.VMEM((2, PIECE_ROWS, LANES), F32),
                pltpu.VMEM((2, PIECE_ROWS, LANES), F32),
                pltpu.VMEM((GROUP, 2, PIECE_ROWS, LANES), F32),
                pltpu.VMEM((COARSE_TILES, 2, ROWS, LANES), F32),
                pltpu.VMEM((RELAYS, 2, RELAY_ROWS, LANES), F32),
                pltpu.VMEM((RELAYS, 2, RELAY_ROWS, LANES), F32),
                dma((TILES, 2)),
                dma((2, 3)),
                dma((2, 3)),
                dma((TILES + 4,)),
                dma,
                dma((GROUP,)),
                dma((GROUP,)),
                dma,
                dma,
                dma((GROUP,)),
                dma((GROUP,)),
                dma((3, RELAYS)),
                dma((2, RELAYS)),
                pltpu.SemaphoreType.REGULAR,
                pltpu.SemaphoreType.REGULAR,
                pltpu.VMEM((2, 2, PIECE_ROWS, LANES), F32),
                dma((2,)),
                dma((2,)),
            ],
            compiler_params=pltpu.CompilerParams(collective_id=0, has_side_effects=True, vmem_limit_bytes=61696 * 1024),
            name="pfasst",
        )(start_values[0], node_values[0].reshape(4, ROWS, KY))
        next_start, nodes = pl.pallas_call(
            deliver,
            out_shape=(jax.ShapeDtypeStruct((2, ROWS, KY), F32), jax.ShapeDtypeStruct((4, ROWS, KY), F32)),
            in_specs=[vmem, vmem],
            out_specs=(hbm, hbm),
            scratch_shapes=[dma((6,))],
            compiler_params=pltpu.CompilerParams(vmem_limit_bytes=2**20),
            name="deliver",
        )(next_start, nodes)
        return next_start[None], nodes.reshape(1, 2, 2, ROWS, KY)

    return jax.shard_map(
        body,
        mesh=mesh,
        in_specs=(P("tm", None, "space", None), P("tm", None, None, "space", None)),
        out_specs=(P("tm", None, "space", None), P("tm", None, None, "space", None)),
        check_vma=False,
    )
```

time: 40.5 us -> 34.1 us (0.84)
  the two profiles are of different devices: /device:TPU:3 before, /device:TPU:196 now
where the time goes in v2:
time: 34.1 us; the launch traced here: 34 us
  Pallas kernels  33.4 us (98%)
  between operations  0.64 us (2%)
    pallas_call x1, Pallas kernels, body(): pl.pallas_call(functools.partial(kernel, tm_size, space_size), out_shape=...  31.7 us
    pallas_call x1, Pallas kernels, body(): pl.pallas_call(deliver, out_shape=(jax.ShapeDtypeStruct((2, ROWS, KY), F3...  1.71 us

profile of v2, /device:TPU:196, one launch (start us, length us, event | category | flops | bytes accessed | tf_op | source)
XLA Modules:
  0.0 34.0 jit_solution(15316838259100458118)
XLA Ops:
  0.6 31.7 %pfasst.1 = (f32[2,128,1024]{2,1,0:T(8,128)S(1)}, f32[4,128,1024]{2,1,0:T(8,128)S(1)}) custom-call(f32[2,128,1024]{2,1,0:T(8,128)} %bitcast.5, f32[4,128,1024]{2,1,0:T(8,128)} %bitcast.4), custom_call_target="tpu_custom_call" | custom-call | tf_op jit(solution)/shard_map/pfasst/pallas_call | solution.py:691
  32.3 1.7 %deliver.1 = (f32[2,128,1024]{2,1,0:T(8,128)}, f32[4,128,1024]{2,1,0:T(8,128)}) custom-call(f32[2,128,1024]{2,1,0:T(8,128)S(1)} %get-tuple-element.6.start_ref, f32[4,128,1024]{2,1,0:T(8,128)S(1)} %get-tuple-element.7.nodes_ref), custom_call_target="tpu_custom_call" | custom-call | tf_op jit(solution)/shard_map/deliver/pallas_call | solution.py:732

commit v3 on v2

--- a/solution.py
+++ b/solution.py
@@ -21,14 +21,21 @@
 COARSE_RANKS = CX // ROWS
 FINE_TILES = TILES - COARSE_TILES
 RING = 4
-GROUP = 16
+GROUP = 8
 PIECE_ROWS = COARSE_TILES * ROWS // GROUP
 RELAY_SHARED = 1
 RELAY_WRAP = 0
-RELAYS = 2 * (2 + RELAY_SHARED + RELAY_WRAP)
+RELAY_BOTH = 1
+RELAYS = 2 * (2 + RELAY_SHARED + RELAY_WRAP + RELAY_BOTH)
 RELAY_ROWS = 56
-EARLY = 5
-EARLY_WRAP = 5
+EARLY = 4
+EARLY_WRAP = 3
+EARLY_STEP = 4
+WRAP_STEP = 3
+LEAD = 1
+ASIDE_GROUPS = 2
+FIRST = 2
+FIRST_WRAP = 1
 
 diffusion = 1.5
 drift = 0.8
@@ -314,7 +321,7 @@
     def _():
         def relay_source(chunk):
             rows = pl.ds(pl.multiple_of(8 + lax.rem(chunk, 2) * RELAY_ROWS, 8), RELAY_ROWS)
-            return rows, columns(tile_at(chunk // 2))
+            return rows, columns(tile_at(LEAD + chunk // 2))
 
         def leg(which, chunk):
             rows, cols = relay_source(chunk)
@@ -333,11 +340,14 @@
         def relayed(which):
             start = lax.rem(place + which, RING)
             wraps = (start == RING - 1).astype(jnp.int32)
-            return 2 + RELAY_SHARED * shared.astype(jnp.int32) + RELAY_WRAP * wraps
+            return 2 + RELAY_WRAP * wraps + count(shared) * (RELAY_SHARED + RELAY_BOTH * wraps)
 
         def has_origin(which):
             return column * RING + lax.rem(place + which, RING) < tm_size - 1
 
+        def aside_tile(index):
+            return (index >= LEAD) & (index < LEAD + relayed(0))
+
         def start_tile(index, carry):
             @pl.when(index >= COARSE_TILES)
             def _():
@@ -345,12 +355,12 @@
 
             inner(tile_at(index))
 
-            @pl.when(has_origin(0) & (index < relayed(0)))
-            def _():
-                leg(0, 2 * index).start()
-                leg(0, 2 * index + 1).start()
-
-            @pl.when(has_origin(0) & (index >= relayed(0)))
+            @pl.when(has_origin(0) & aside_tile(index))
+            def _():
+                leg(0, 2 * (index - LEAD)).start()
+                leg(0, 2 * (index - LEAD) + 1).start()
+
+            @pl.when(has_origin(0) & jnp.logical_not(aside_tile(index)))
             def _():
                 bulk(middle, columns(tile_at(index)), index).start()
 
@@ -397,7 +407,7 @@
         @pl.when(slot < tm_size - 1)
         def _():
             def sent(index, carry):
-                @pl.when(index >= relayed(0))
+                @pl.when(jnp.logical_not(aside_tile(index)))
                 def _():
                     bulk(middle, columns(tile_at(index)), index).wait_send()
 
@@ -428,10 +438,6 @@
             rows = pl.ds(pl.multiple_of(lax.rem(number, share) * PIECE_ROWS, 8), PIECE_ROWS)
             return number // share, slice(None), rows, slice(None)
 
-        def inner_only(index, carry):
-            inner(tile_at(index))
-            return carry
-
         def push_only(index, carry):
             push(middle, columns(tile_at(index)), index)
             return carry
@@ -439,7 +445,17 @@
         lax.fori_loop(COARSE_TILES, TILES, lambda index, carry: (wait_load(tile_at(index)), carry)[1], 0)
         send_halo(1, 2)
         with jax.named_scope("innerA"):
-            lax.fori_loop(COARSE_TILES, TILES, inner_only, 0)
+            def inner_and_push(index, carry):
+                inner(tile_at(index))
+
+                @pl.when(index < first_pushes)
+                def _():
+                    push_only(index, 0)
+
+                return carry
+
+            first_pushes = COARSE_TILES + jnp.where(place == RING - 1, FIRST_WRAP, FIRST)
+            lax.fori_loop(COARSE_TILES, TILES, inner_and_push, 0)
         with jax.named_scope("halo"):
             wait_halo(0)
 
@@ -493,14 +509,17 @@
                 src_ref=aside.at[stage], dst_ref=target, send_sem=aside_send.at[stage], recv_sem=sem.at[origin],
                 device_id=in_group(beside_row), device_id_type=MESH)
 
+        def crowded(stage):
+            return group >= 0 if stage == 0 else group < ASIDE_GROUPS
+
         def pass_aside(stage):
-            @pl.when(place == 0)
+            @pl.when((place == 0) & crowded(stage))
             def _():
                 detour(stage).wait_recv()
                 relay_aside(stage).start()
 
-        def blocked(target):
-            return (place == RING - 1) & (target == row * RING)
+        def blocked(target, stage):
+            return (place == RING - 1) & (target == row * RING) & crowded(stage)
 
         def other(distance):
             return lax.rem(member + distance, GROUP)
@@ -513,7 +532,7 @@
                 pl.semaphore_wait(ready, GROUP - 1 - member)
 
         def spread(distance, carry):
-            @pl.when(jnp.logical_not(blocked(other(distance))))
+            @pl.when(jnp.logical_not(blocked(other(distance), 0)))
             def _():
                 gather(member, other(distance)).start()
 
@@ -526,8 +545,14 @@
 
             lax.fori_loop(1, GROUP, spread, 0)
         gathered[member] = offset[piece(member)]
-        early = jnp.where(place == RING - 1, EARLY_WRAP, EARLY)
-        lax.fori_loop(COARSE_TILES, early, push_only, 0)
+        early = jnp.where(place == RING - 1, EARLY_WRAP + group * WRAP_STEP // 2, EARLY + group * EARLY_STEP // 2)
+        early = jnp.minimum(early, TILES)
+        early = jnp.maximum(early, first_pushes)
+        lax.fori_loop(first_pushes, early, push_only, 0)
+        with jax.named_scope("halo2"):
+            wait_halo(1, 2)
+        with jax.named_scope("rim"):
+            lax.fori_loop(COARSE_TILES, TILES, edge, 0)
         tile, _, _, _ = piece(member)
         number = jnp.where(lax.rem(group, 2) == 1, depth - 1 - member // RING, member // RING) * RING + place
         first = lax.rem(number, GROUP // COARSE_TILES) * PIECE_ROWS
@@ -568,24 +593,20 @@
                 hand_on().start()
 
         def give(distance, carry):
-            @pl.when(jnp.logical_not(blocked(other(distance))))
+            @pl.when(jnp.logical_not(blocked(other(distance), 1)))
             def _():
                 scatter(member, other(distance)).start()
 
             return carry
 
         with jax.named_scope("give"):
-            @pl.when(place == RING - 1)
+            @pl.when((place == RING - 1) & crowded(1))
             def _():
                 detour(1).start()
 
             lax.fori_loop(1, GROUP, give, 0)
         begins[piece(member)] = results[member]
         lax.fori_loop(early, TILES, push_only, 0)
-        with jax.named_scope("halo2"):
-            wait_halo(1, 2)
-        with jax.named_scope("rim"):
-            lax.fori_loop(COARSE_TILES, TILES, edge, 0)
         left = pl.ds(0, FIRST_COARSE_TILE * LANES)
         right_start = (FIRST_COARSE_TILE + COARSE_TILES) * LANES
         right = pl.ds(right_start, KY - right_start)
@@ -647,9 +668,9 @@
 
         lax.fori_loop(1, GROUP, let_go, 0)
 
-        @pl.when(place == 0)
-        def _():
-            for stage in range(2):
+        for stage in range(2):
+            @pl.when((place == 0) & crowded(stage))
+            def _():
                 relay_aside(stage).wait_send()
 
     @pl.when(rank < space_size - 1)

time: 34.1 us -> 30.9 us (0.906)
  the two profiles are of different devices: /device:TPU:196 before, /device:TPU:228 now
where the time goes in v3:
time: 30.9 us; the launch traced here: 30.8 us
  Pallas kernels  30.1 us (97%)
  between operations  0.64 us (2%)
    pallas_call x1, Pallas kernels, body(): pl.pallas_call(functools.partial(kernel, tm_size, space_size), out_shape=...  28.4 us
    pallas_call x1, Pallas kernels, body(): pl.pallas_call(deliver, out_shape=(jax.ShapeDtypeStruct((2, ROWS, KY), F3...  1.71 us

profile of v3, /device:TPU:228, one launch (start us, length us, event | category | flops | bytes accessed | tf_op | source)
XLA Modules:
  0.0 30.8 jit_solution(12427349371741647212)
XLA Ops:
  0.6 28.4 %pfasst.1 = (f32[2,128,1024]{2,1,0:T(8,128)S(1)}, f32[4,128,1024]{2,1,0:T(8,128)S(1)}) custom-call(f32[2,128,1024]{2,1,0:T(8,128)} %bitcast.5, f32[4,128,1024]{2,1,0:T(8,128)} %bitcast.4), custom_call_target="tpu_custom_call" | custom-call | tf_op jit(solution)/shard_map/pfasst/pallas_call | solution.py:712
  29.0 1.7 %deliver.1 = (f32[2,128,1024]{2,1,0:T(8,128)}, f32[4,128,1024]{2,1,0:T(8,128)}) custom-call(f32[2,128,1024]{2,1,0:T(8,128)S(1)} %get-tuple-element.6.start_ref, f32[4,128,1024]{2,1,0:T(8,128)S(1)} %get-tuple-element.7.nodes_ref), custom_call_target="tpu_custom_call" | custom-call | tf_op jit(solution)/shard_map/deliver/pallas_call | solution.py:753

commit v4 on v3

--- a/solution.py
+++ b/solution.py
@@ -24,18 +24,20 @@
 GROUP = 8
 PIECE_ROWS = COARSE_TILES * ROWS // GROUP
 RELAY_SHARED = 1
-RELAY_WRAP = 0
+RELAY_WRAP = 1
 RELAY_BOTH = 1
 RELAYS = 2 * (2 + RELAY_SHARED + RELAY_WRAP + RELAY_BOTH)
 RELAY_ROWS = 56
 EARLY = 4
-EARLY_WRAP = 3
-EARLY_STEP = 4
-WRAP_STEP = 3
+EARLY_WRAP = 5
+EARLY_STEP = 2
+WRAP_STEP = 2
 LEAD = 1
+EARLY_ZERO = 2
+LAG = 6
 ASIDE_GROUPS = 2
 FIRST = 2
-FIRST_WRAP = 1
+FIRST_WRAP = 2
 
 diffusion = 1.5
 drift = 0.8
@@ -69,7 +71,7 @@
 
 
 def kernel(tm_size, space_size, start_hbm, nodes_hbm, next_out, nodes_out, fields, mixed, staged, node_one_buf, whole, offset,
-           gathered, carry_in, carry_out, results, begins, first_leg, second_leg, load_sem, halo_send, halo_recv, bulk_send,
+           gathered, prefix, carry_in, carry_out, results, begins, first_leg, second_leg, load_sem, halo_send, halo_recv, bulk_send,
            bulk_recv, gather_send, gather_recv, carry_send, carry_recv, scatter_send, scatter_recv, relay_send, relay_recv,
            ready, ready_carry, aside, aside_send, aside_recv):
     slot = lax.axis_index("tm")
@@ -90,13 +92,13 @@
     def loads(tile):
         body = pl.ds(8, ROWS)
         return (
-            pltpu.make_async_copy(start_hbm.at[:, :, columns(tile)], fields.at[tile, pl.ds(0, 2), body, :], load_sem.at[tile, 0]),
-            pltpu.make_async_copy(nodes_hbm.at[:, :, columns(tile)], fields.at[tile, pl.ds(2, 4), body, :], load_sem.at[tile, 1]),
+            pltpu.make_async_copy(start_hbm.at[:, :, columns(tile)], fields.at[tile, pl.ds(0, 2), body, :], load_sem.at[tile]),
+            pltpu.make_async_copy(nodes_hbm.at[:, :, columns(tile)], fields.at[tile, pl.ds(2, 4), body, :], load_sem.at[tile]),
         )
 
     def wait_load(tile):
-        for copy in loads(tile):
-            copy.wait()
+        landed = fields.at[tile, :, pl.ds(8, ROWS), :]
+        pltpu.make_async_copy(landed, landed, load_sem.at[tile]).wait()
 
     barrier = pltpu.get_barrier_semaphore()
 
@@ -123,13 +125,11 @@
 
     member, group = lax.rem(slot, GROUP), slot // GROUP
     groups = tm_size // GROUP
-    depth = GROUP // RING
-
     def in_group(index):
         return at_slot(group * GROUP + index)
 
-    def facing(step):
-        return at_slot((group + step) * GROUP + (depth - 1 - member // RING) * RING + place)
+    def facing(index):
+        return at_slot(index * GROUP + member)
 
     @pl.when(coarse)
     def _():
@@ -139,9 +139,11 @@
 
         lax.fori_loop(member + 1, GROUP, call, 0)
 
-        @pl.when(group < groups - 1)
-        def _():
-            greet(facing(1))
+        def call_later(index, carry):
+            greet(facing(index))
+            return carry
+
+        lax.fori_loop(group + 1, groups, call_later, 0)
 
     def begin_load(index, carry):
         for copy in loads(tile_at(index)):
@@ -160,14 +162,16 @@
         return flag.astype(jnp.int32)
 
     with jax.named_scope("barrier"):
-        own_kind = jnp.where(coarse, member + count(group > 0), 1 + count(place == 1))
+        own_kind = jnp.where(coarse, member + group, 1 + count(place == 1))
         pl.semaphore_wait(barrier, 1 + count(rank > 0) + count(rank < space_size - 1) + own_kind)
 
     @pl.when(coarse)
     def _():
-        @pl.when(group > 0)
-        def _():
-            pl.semaphore_signal(ready_carry, inc=1, device_id=facing(-1), device_id_type=MESH)
+        def answer_earlier(index, carry):
+            pl.semaphore_signal(ready_carry, inc=1, device_id=facing(index), device_id_type=MESH)
+            return carry
+
+        lax.fori_loop(0, group, answer_earlier, 0)
 
         def answer(index, carry):
             pl.semaphore_signal(ready, inc=1, device_id=in_group(index), device_id_type=MESH)
@@ -182,7 +186,7 @@
         low, high = (ROWS, 0) if side == 0 else (8, ROWS + 8)
         return pltpu.make_async_remote_copy(
             src_ref=fields.at[parts[part], :, pl.ds(low, 8), :], dst_ref=fields.at[parts[part], :, pl.ds(high, 8), :],
-            send_sem=halo_send.at[side, part], recv_sem=halo_recv.at[side, part],
+            send_sem=halo_send.at[side], recv_sem=halo_recv.at[side, part],
             device_id={"tm": slot, "space": rank + 1 if side == 0 else rank - 1}, device_id_type=MESH)
 
     def send_halo(*which):
@@ -206,6 +210,21 @@
         def _():
             for part in which:
                 halo(1, part).wait_recv()
+
+    def all_of(ref, send, recv):
+        return pltpu.make_async_remote_copy(
+            src_ref=ref, dst_ref=ref, send_sem=send, recv_sem=recv, device_id=at_slot(after), device_id_type=MESH)
+
+    def halo_sent():
+        edge_rows = fields.at[:, :, pl.ds(0, 8), :]
+
+        @pl.when(rank < space_size - 1)
+        def _():
+            all_of(edge_rows, halo_send.at[0], halo_recv.at[0, 0]).wait_send()
+
+        @pl.when(rank > 0)
+        def _():
+            all_of(edge_rows, halo_send.at[1], halo_recv.at[0, 0]).wait_send()
 
     send_halo(0)
 
@@ -214,7 +233,7 @@
             src_ref=nodes_out.at[pl.ds(2, 2), rows, cols], dst_ref=next_out.at[:, rows, cols],
             send_sem=bulk_send.at[index], recv_sem=bulk_recv, device_id=at_slot(after), device_id_type=MESH)
 
-    def push(rows, cols, index):
+    def push(rows, cols, index=0):
         @pl.when(slot < tm_size - 1)
         def _():
             bulk(rows, cols, index).start()
@@ -301,13 +320,6 @@
     upper = pl.ds(0, 8)
     lower = pl.ds(120, 8)
 
-    def inner_push(index, carry):
-        tile = tile_at(index)
-        wait_load(tile)
-        inner(tile)
-        push(middle, columns(tile), index)
-        return carry
-
     def edge(index, carry):
         rim(tile_at(index))
         return carry
@@ -334,7 +346,7 @@
                 origin = column * RING + lax.rem(place + 2, RING)
                 source, target, device, recv = second_leg.at[chunk], next_out.at[:, rows, cols], at_slot(origin + 1), bulk_recv
             return pltpu.make_async_remote_copy(
-                src_ref=source, dst_ref=target, send_sem=relay_send.at[which, chunk], recv_sem=recv,
+                src_ref=source, dst_ref=target, send_sem=relay_send.at[which], recv_sem=recv,
                 device_id=device, device_id_type=MESH)
 
         def relayed(which):
@@ -362,12 +374,12 @@
 
             @pl.when(has_origin(0) & jnp.logical_not(aside_tile(index)))
             def _():
-                bulk(middle, columns(tile_at(index)), index).start()
+                bulk(middle, columns(tile_at(index))).start()
 
             return carry
 
         def forward(which, chunk):
-            @pl.when(has_origin(which) & (chunk < 2 * relayed(which)))
+            @pl.when(has_origin(which) & (chunk >= 0) & (chunk < 2 * relayed(which)))
             def _():
                 leg(which - 1, chunk).wait_recv()
                 leg(which, chunk).start()
@@ -391,55 +403,50 @@
 
         with jax.named_scope("rim"):
             lax.fori_loop(0, TILES, edge, 0)
-        push(upper, slice(None), TILES)
-        push(lower, slice(None), TILES + 1)
+        push(upper, slice(None), 1)
+        push(lower, slice(None), 1)
 
         def pass_on(step, carry):
             forward(1, step)
-            forward(2, step - 2)
+            forward(2, step - LAG)
             return carry
 
         with jax.named_scope("fwdB"):
-            lax.fori_loop(2, RELAYS + 2, pass_on, 0)
+            lax.fori_loop(2, RELAYS + LAG, pass_on, 0)
+        halo_sent()
+
+        def tiles_sent(relays):
+            return bulk(middle, pl.ds(0, (TILES - relays) * LANES)), first_leg.at[pl.ds(0, 2 * relays)]
+
+        for relays in range(2, RELAYS // 2 + 1):
+            direct, chunks = tiles_sent(relays)
+            for which in range(3):
+                @pl.when(has_origin(which) & (relayed(which) == relays))
+                def _():
+                    all_of(chunks, relay_send.at[which], relay_recv.at[0, 0]).wait_send()
+
+            @pl.when(has_origin(0) & (relayed(0) == relays))
+            def _():
+                direct.wait_send()
+
+        @pl.when(has_origin(0))
+        def _():
+            bulk(pl.ds(0, 16), slice(None), 1).wait_send()
+
         with jax.named_scope("settle"):
             settle(slice(None))
-
-        @pl.when(slot < tm_size - 1)
-        def _():
-            def sent(index, carry):
-                @pl.when(jnp.logical_not(aside_tile(index)))
-                def _():
-                    bulk(middle, columns(tile_at(index)), index).wait_send()
-
-                return carry
-
-            lax.fori_loop(0, TILES, sent, 0)
-            bulk(upper, slice(None), TILES).wait_send()
-            bulk(lower, slice(None), TILES + 1).wait_send()
-
-        for which in range(3):
-            def legs_sent(chunk, carry):
-                @pl.when(has_origin(which) & (chunk < 2 * relayed(which)))
-                def _():
-                    leg(which, chunk).wait_send()
-
-                return carry
-
-            lax.fori_loop(0, RELAYS, legs_sent, 0)
 
     @pl.when(coarse)
     def _():
         lead = (slot == 0).astype(F32)
 
         def piece(index):
-            row = index // RING
-            number = jnp.where(lax.rem(group, 2) == 1, depth - 1 - row, row) * RING + lax.rem(index, RING)
             share = GROUP // COARSE_TILES
-            rows = pl.ds(pl.multiple_of(lax.rem(number, share) * PIECE_ROWS, 8), PIECE_ROWS)
-            return number // share, slice(None), rows, slice(None)
+            rows = pl.ds(pl.multiple_of(lax.rem(index, share) * PIECE_ROWS, 8), PIECE_ROWS)
+            return index // share, slice(None), rows, slice(None)
 
         def push_only(index, carry):
-            push(middle, columns(tile_at(index)), index)
+            push(middle, columns(tile_at(index)))
             return carry
 
         lax.fori_loop(COARSE_TILES, TILES, lambda index, carry: (wait_load(tile_at(index)), carry)[1], 0)
@@ -478,18 +485,18 @@
 
         def gather(source, target):
             return pltpu.make_async_remote_copy(
-                src_ref=offset.at[piece(target)], dst_ref=gathered.at[source], send_sem=gather_send.at[target],
-                recv_sem=gather_recv.at[source], device_id=in_group(target), device_id_type=MESH)
+                src_ref=offset.at[piece(target)], dst_ref=gathered.at[source], send_sem=gather_send,
+                recv_sem=gather_recv, device_id=in_group(target), device_id_type=MESH)
 
         def scatter(source, target):
             return pltpu.make_async_remote_copy(
-                src_ref=results.at[target], dst_ref=begins.at[piece(source)], send_sem=scatter_send.at[target],
-                recv_sem=scatter_recv.at[source], device_id=in_group(target), device_id_type=MESH)
-
-        def hand_on():
+                src_ref=results.at[target], dst_ref=begins.at[piece(source)], send_sem=scatter_send,
+                recv_sem=scatter_recv, device_id=in_group(target), device_id_type=MESH)
+
+        def hand_on(source, target):
             return pltpu.make_async_remote_copy(
-                src_ref=carry_out, dst_ref=carry_in, send_sem=carry_send, recv_sem=carry_recv, device_id=facing(1),
-                device_id_type=MESH)
+                src_ref=carry_out, dst_ref=carry_in.at[source], send_sem=carry_send,
+                recv_sem=carry_recv, device_id=facing(target), device_id_type=MESH)
 
         row = member // RING
         beside_row = (row + 1 - 2 * lax.rem(row, 2)) * RING
@@ -498,7 +505,7 @@
             source = offset.at[piece(row * RING)] if stage == 0 else results.at[row * RING]
             sem = gather_send if stage == 0 else scatter_send
             return pltpu.make_async_remote_copy(
-                src_ref=source, dst_ref=aside.at[stage], send_sem=sem.at[row * RING], recv_sem=aside_recv.at[stage],
+                src_ref=source, dst_ref=aside.at[stage], send_sem=sem, recv_sem=aside_recv.at[stage],
                 device_id=in_group(beside_row), device_id_type=MESH)
 
         def relay_aside(stage):
@@ -506,7 +513,7 @@
             target = gathered.at[origin] if stage == 0 else begins.at[piece(origin)]
             sem = gather_recv if stage == 0 else scatter_recv
             return pltpu.make_async_remote_copy(
-                src_ref=aside.at[stage], dst_ref=target, send_sem=aside_send.at[stage], recv_sem=sem.at[origin],
+                src_ref=aside.at[stage], dst_ref=target, send_sem=aside_send.at[stage], recv_sem=sem,
                 device_id=in_group(beside_row), device_id_type=MESH)
 
         def crowded(stage):
@@ -520,6 +527,8 @@
 
         def blocked(target, stage):
             return (place == RING - 1) & (target == row * RING) & crowded(stage)
+
+        others = gathered.at[pl.ds(0, GROUP - 1)]
 
         def other(distance):
             return lax.rem(member + distance, GROUP)
@@ -545,7 +554,7 @@
 
             lax.fori_loop(1, GROUP, spread, 0)
         gathered[member] = offset[piece(member)]
-        early = jnp.where(place == RING - 1, EARLY_WRAP + group * WRAP_STEP // 2, EARLY + group * EARLY_STEP // 2)
+        early = jnp.where(place == RING - 1, EARLY_WRAP + group * WRAP_STEP // 2, EARLY + count(place == 0) * EARLY_ZERO + group * EARLY_STEP // 2)
         early = jnp.minimum(early, TILES)
         early = jnp.maximum(early, first_pushes)
         lax.fori_loop(first_pushes, early, push_only, 0)
@@ -553,75 +562,86 @@
             wait_halo(1, 2)
         with jax.named_scope("rim"):
             lax.fori_loop(COARSE_TILES, TILES, edge, 0)
-        tile, _, _, _ = piece(member)
-        number = jnp.where(lax.rem(group, 2) == 1, depth - 1 - member // RING, member // RING) * RING + place
-        first = lax.rem(number, GROUP // COARSE_TILES) * PIECE_ROWS
-        rate_real, rate_imag, _ = rate_of(rank * ROWS + first, (FIRST_COARSE_TILE + tile) * LANES, PIECE_ROWS)
-        gain = inverse(1.0 - rate_real, -rate_imag)
-
-        with jax.named_scope("aside0"):
-            pass_aside(0)
-        with jax.named_scope("gather"):
-            def arrive(distance, carry):
-                gather(other(distance), member).wait_recv()
-                return carry
-
-            lax.fori_loop(1, GROUP, arrive, 0)
-
-        with jax.named_scope("carry"):
-            @pl.when(group == 0)
-            def _():
-                carry_in[...] = jnp.zeros((2, PIECE_ROWS, LANES), F32)
-
-            @pl.when(group > 0)
-            def _():
-                hand_on().wait_recv()
-
-        def scan(index, running):
-            for i in range(2):
-                results[index, i] = running[i]
-            return times(*gain, running[0] + gathered[index, 0], running[1] + gathered[index, 1])
-
-        with jax.named_scope("scan"):
-            running = lax.fori_loop(0, GROUP, scan, (carry_in[0], carry_in[1]))
-            for i in range(2):
-                carry_out[i] = running[i]
-
-            @pl.when(group < groups - 1)
-            def _():
-                pl.semaphore_wait(ready_carry, 1)
-                hand_on().start()
-
-        def give(distance, carry):
-            @pl.when(jnp.logical_not(blocked(other(distance), 1)))
-            def _():
-                scatter(member, other(distance)).start()
-
-            return carry
-
-        with jax.named_scope("give"):
-            @pl.when((place == RING - 1) & crowded(1))
-            def _():
-                detour(1).start()
-
-            lax.fori_loop(1, GROUP, give, 0)
-        begins[piece(member)] = results[member]
-        lax.fori_loop(early, TILES, push_only, 0)
         left = pl.ds(0, FIRST_COARSE_TILE * LANES)
         right_start = (FIRST_COARSE_TILE + COARSE_TILES) * LANES
         right = pl.ds(right_start, KY - right_start)
         rims = [(upper, left), (upper, right), (lower, left), (lower, right)]
-        for number, (rows, cols) in enumerate(rims):
-            push(rows, cols, TILES + number)
+        for rows, cols in rims:
+            push(rows, cols, 1)
+        tile, _, _, _ = piece(member)
+        first = lax.rem(member, GROUP // COARSE_TILES) * PIECE_ROWS
+        rate_real, rate_imag, _ = rate_of(rank * ROWS + first, (FIRST_COARSE_TILE + tile) * LANES, PIECE_ROWS)
+        gain = inverse(1.0 - rate_real, -rate_imag)
+
+        with jax.named_scope("aside0"):
+            pass_aside(0)
+        with jax.named_scope("gather"):
+            all_of(others, gather_send, gather_recv).wait_recv()
+
+        def scan(index, running):
+            for i in range(2):
+                prefix[index, i] = running[i]
+            return times(*gain, running[0] + gathered[index, 0], running[1] + gathered[index, 1])
+
+        nothing = jnp.zeros((PIECE_ROWS, LANES), F32)
+        with jax.named_scope("scan"):
+            running = lax.fori_loop(0, GROUP, scan, (nothing, nothing))
+            for i in range(2):
+                carry_out[i] = running[i]
+
+            @pl.when(group < groups - 1)
+            def _():
+                pl.semaphore_wait(ready_carry, groups - 1 - group)
+
+            def tell(target, carry):
+                hand_on(group, target).start()
+                return carry
+
+            lax.fori_loop(group + 1, groups, tell, 0)
+
+        jump = gain
+        for _ in range(GROUP.bit_length() - 1):
+            jump = times(*jump, *jump)
+
+        def join(source, running):
+            far = times(*jump, *running)
+            return far[0] + carry_in[source, 0], far[1] + carry_in[source, 1]
+
+        with jax.named_scope("carry"):
+            for number in range(1, groups):
+                @pl.when(group == number)
+                def _():
+                    all_of(carry_in.at[pl.ds(0, number)], carry_send, carry_recv).wait_recv()
+
+            entering = lax.fori_loop(0, group, join, (nothing, nothing))
+
+        def add_carry(index, running):
+            for i in range(2):
+                results[index, i] = prefix[index, i] + running[i]
+            return times(*gain, *running)
+
+        lax.fori_loop(0, GROUP, add_carry, entering)
+
+        def give(distance, carry):
+            @pl.when(jnp.logical_not(blocked(other(distance), 1)))
+            def _():
+                scatter(member, other(distance)).start()
+
+            return carry
+
+        with jax.named_scope("give"):
+            @pl.when((place == RING - 1) & crowded(1))
+            def _():
+                detour(1).start()
+
+            lax.fori_loop(1, GROUP, give, 0)
+        begins[piece(member)] = results[member]
+        lax.fori_loop(early, TILES, push_only, 0)
 
         with jax.named_scope("aside1"):
             pass_aside(1)
         with jax.named_scope("back"):
-            def fetch(distance, carry):
-                scatter(other(distance), member).wait_recv()
-                return carry
-
-            lax.fori_loop(1, GROUP, fetch, 0)
+            all_of(others, scatter_send, scatter_recv).wait_recv()
 
         later = 1.0 - lead
 
@@ -644,44 +664,28 @@
         with jax.named_scope("finish"):
             lax.fori_loop(FIRST_COARSE_TILE, FIRST_COARSE_TILE + COARSE_TILES, finish, 0)
 
+        halo_sent()
+
+        for number in range(1, groups):
+            @pl.when(group == groups - 1 - number)
+            def _():
+                all_of(carry_in.at[pl.ds(0, number)], carry_send, carry_recv).wait_send()
+
+        all_of(others, gather_send, gather_recv).wait_send()
+        all_of(others, scatter_send, scatter_recv).wait_send()
+
+        for stage in range(2):
+            @pl.when((place == 0) & crowded(stage))
+            def _():
+                relay_aside(stage).wait_send()
+
+        @pl.when(slot < tm_size - 1)
+        def _():
+            bulk(middle, pl.ds(0, FINE_TILES * LANES)).wait_send()
+            bulk(pl.ds(0, 16), pl.ds(0, FINE_TILES * LANES), 1).wait_send()
+
         with jax.named_scope("settle"):
             settle(pl.ds(0, FINE_TILES * LANES))
-
-        @pl.when(slot < tm_size - 1)
-        def _():
-            def sent(index, carry):
-                bulk(middle, columns(tile_at(index)), index).wait_send()
-                return carry
-
-            lax.fori_loop(COARSE_TILES, TILES, sent, 0)
-            for number, (rows, cols) in enumerate(rims):
-                bulk(rows, cols, TILES + number).wait_send()
-
-        @pl.when(group < groups - 1)
-        def _():
-            hand_on().wait_send()
-
-        def let_go(distance, carry):
-            gather(member, other(distance)).wait_send()
-            scatter(member, other(distance)).wait_send()
-            return carry
-
-        lax.fori_loop(1, GROUP, let_go, 0)
-
-        for stage in range(2):
-            @pl.when((place == 0) & crowded(stage))
-            def _():
-                relay_aside(stage).wait_send()
-
-    @pl.when(rank < space_size - 1)
-    def _():
-        for part in range(3):
-            halo(0, part).wait_send()
-
-    @pl.when(rank > 0)
-    def _():
-        for part in range(3):
-            halo(1, part).wait_send()
 
     @pl.when(slot == 0)
     def _():
@@ -722,24 +726,25 @@
                 pltpu.VMEM((2, ROWS + 32, LANES), F32),
                 pltpu.VMEM((COARSE_TILES, 2, ROWS, LANES), F32),
                 pltpu.VMEM((GROUP, 2, PIECE_ROWS, LANES), F32),
-                pltpu.VMEM((2, PIECE_ROWS, LANES), F32),
+                pltpu.VMEM((GROUP, 2, PIECE_ROWS, LANES), F32),
+                pltpu.VMEM((tm_size // GROUP, 2, PIECE_ROWS, LANES), F32),
                 pltpu.VMEM((2, PIECE_ROWS, LANES), F32),
                 pltpu.VMEM((GROUP, 2, PIECE_ROWS, LANES), F32),
                 pltpu.VMEM((COARSE_TILES, 2, ROWS, LANES), F32),
                 pltpu.VMEM((RELAYS, 2, RELAY_ROWS, LANES), F32),
                 pltpu.VMEM((RELAYS, 2, RELAY_ROWS, LANES), F32),
-                dma((TILES, 2)),
+                dma((TILES,)),
+                dma((2,)),
                 dma((2, 3)),
-                dma((2, 3)),
-                dma((TILES + 4,)),
-                dma,
-                dma((GROUP,)),
-                dma((GROUP,)),
+                dma((2,)),
                 dma,
                 dma,
-                dma((GROUP,)),
-                dma((GROUP,)),
-                dma((3, RELAYS)),
+                dma,
+                dma,
+                dma,
+                dma,
+                dma,
+                dma((3,)),
                 dma((2, RELAYS)),
                 pltpu.SemaphoreType.REGULAR,
                 pltpu.SemaphoreType.REGULAR,

time: 30.9 us -> 28.3 us (0.916)
  the two profiles are of different devices: /device:TPU:228 before, /device:TPU:196 now
where the time goes in v4:
time: 28.3 us; the launch traced here: 27.9 us
  Pallas kernels  27.3 us (96%)
  between operations  0.64 us (2%)
    pallas_call x1, Pallas kernels, body(): pl.pallas_call(functools.partial(kernel, tm_size, space_size), out_shape=...  25.6 us
    pallas_call x1, Pallas kernels, body(): pl.pallas_call(deliver, out_shape=(jax.ShapeDtypeStruct((2, ROWS, KY), F3...  1.71 us

profile of v4, /device:TPU:196, one launch (start us, length us, event | category | flops | bytes accessed | tf_op | source)
XLA Modules:
  0.0 27.9 jit_solution(4535664807984927050)
XLA Ops:
  0.6 25.6 %pfasst.1 = (f32[2,128,1024]{2,1,0:T(8,128)S(1)}, f32[4,128,1024]{2,1,0:T(8,128)S(1)}) custom-call(f32[2,128,1024]{2,1,0:T(8,128)} %bitcast.5, f32[4,128,1024]{2,1,0:T(8,128)} %bitcast.4), custom_call_target="tpu_custom_call" | custom-call | tf_op jit(solution)/shard_map/pfasst/pallas_call | solution.py:716
  26.2 1.7 %deliver.1 = (f32[2,128,1024]{2,1,0:T(8,128)}, f32[4,128,1024]{2,1,0:T(8,128)}) custom-call(f32[2,128,1024]{2,1,0:T(8,128)S(1)} %get-tuple-element.6.start_ref, f32[4,128,1024]{2,1,0:T(8,128)S(1)} %get-tuple-element.7.nodes_ref), custom_call_target="tpu_custom_call" | custom-call | tf_op jit(solution)/shard_map/deliver/pallas_call | solution.py:758

commit v5 on v4

--- a/solution.py
+++ b/solution.py
@@ -23,19 +23,21 @@
 RING = 4
 GROUP = 8
 PIECE_ROWS = COARSE_TILES * ROWS // GROUP
-RELAY_SHARED = 1
+RELAY_SHARED = 2
 RELAY_WRAP = 1
-RELAY_BOTH = 1
-RELAYS = 2 * (2 + RELAY_SHARED + RELAY_WRAP + RELAY_BOTH)
+RELAY_BOTH = 3
+RELAYS = 4 + RELAY_SHARED + RELAY_WRAP + RELAY_BOTH
 RELAY_ROWS = 56
 EARLY = 4
 EARLY_WRAP = 5
-EARLY_STEP = 2
-WRAP_STEP = 2
+EARLY_STEP = 1
+WRAP_STEP = 1
+LAST_WRAP = 2
+LAST_FIRST = 0
 LEAD = 1
+DELIVER_ROWS = 32
 EARLY_ZERO = 2
 LAG = 6
-ASIDE_GROUPS = 2
 FIRST = 2
 FIRST_WRAP = 2
 
@@ -352,34 +354,40 @@
         def relayed(which):
             start = lax.rem(place + which, RING)
             wraps = (start == RING - 1).astype(jnp.int32)
-            return 2 + RELAY_WRAP * wraps + count(shared) * (RELAY_SHARED + RELAY_BOTH * wraps)
+            return 4 + RELAY_WRAP * wraps + count(shared) * (RELAY_SHARED + RELAY_BOTH * wraps)
 
         def has_origin(which):
             return column * RING + lax.rem(place + which, RING) < tm_size - 1
 
-        def aside_tile(index):
-            return (index >= LEAD) & (index < LEAD + relayed(0))
-
         def start_tile(index, carry):
             @pl.when(index >= COARSE_TILES)
             def _():
                 wait_load(tile_at(index))
 
             inner(tile_at(index))
-
-            @pl.when(has_origin(0) & aside_tile(index))
-            def _():
-                leg(0, 2 * (index - LEAD)).start()
-                leg(0, 2 * (index - LEAD) + 1).start()
-
-            @pl.when(has_origin(0) & jnp.logical_not(aside_tile(index)))
+            first = 2 * (index - LEAD)
+            chunks = jnp.where(first < 0, 0, relayed(0) - first)
+
+            @pl.when(has_origin(0) & (chunks > 0))
+            def _():
+                leg(0, first).start()
+
+            @pl.when(has_origin(0) & (chunks > 1))
+            def _():
+                leg(0, first + 1).start()
+
+            @pl.when(has_origin(0) & (chunks == 1))
+            def _():
+                bulk(pl.ds(8 + RELAY_ROWS, RELAY_ROWS), columns(tile_at(index))).start()
+
+            @pl.when(has_origin(0) & (chunks <= 0))
             def _():
                 bulk(middle, columns(tile_at(index))).start()
 
             return carry
 
         def forward(which, chunk):
-            @pl.when(has_origin(which) & (chunk >= 0) & (chunk < 2 * relayed(which)))
+            @pl.when(has_origin(which) & (chunk >= 0) & (chunk < relayed(which)))
             def _():
                 leg(which - 1, chunk).wait_recv()
                 leg(which, chunk).start()
@@ -415,11 +423,9 @@
             lax.fori_loop(2, RELAYS + LAG, pass_on, 0)
         halo_sent()
 
-        def tiles_sent(relays):
-            return bulk(middle, pl.ds(0, (TILES - relays) * LANES)), first_leg.at[pl.ds(0, 2 * relays)]
-
-        for relays in range(2, RELAYS // 2 + 1):
-            direct, chunks = tiles_sent(relays)
+        for relays in range(4, RELAYS + 1):
+            chunks = first_leg.at[pl.ds(0, relays)]
+            direct = fields.at[pl.ds(0, 7), pl.ds(0, 2), pl.ds(0, 8 * (2 * TILES - relays)), :]
             for which in range(3):
                 @pl.when(has_origin(which) & (relayed(which) == relays))
                 def _():
@@ -427,7 +433,7 @@
 
             @pl.when(has_origin(0) & (relayed(0) == relays))
             def _():
-                direct.wait_send()
+                all_of(direct, bulk_send.at[0], relay_recv.at[0, 0]).wait_send()
 
         @pl.when(has_origin(0))
         def _():
@@ -461,7 +467,7 @@
 
                 return carry
 
-            first_pushes = COARSE_TILES + jnp.where(place == RING - 1, FIRST_WRAP, FIRST)
+            first_pushes = COARSE_TILES + jnp.where(place == RING - 1, FIRST_WRAP + LAST_FIRST * count(group == groups - 1), FIRST)
             lax.fori_loop(COARSE_TILES, TILES, inner_and_push, 0)
         with jax.named_scope("halo"):
             wait_halo(0)
@@ -516,17 +522,17 @@
                 src_ref=aside.at[stage], dst_ref=target, send_sem=aside_send.at[stage], recv_sem=sem,
                 device_id=in_group(beside_row), device_id_type=MESH)
 
-        def crowded(stage):
-            return group >= 0 if stage == 0 else group < ASIDE_GROUPS
+        def crowded(stage, row):
+            return (group > 0) & (row == 0) if stage == 0 else (group == 0) & (row == 1)
 
         def pass_aside(stage):
-            @pl.when((place == 0) & crowded(stage))
+            @pl.when((place == 0) & crowded(stage, 1 - row))
             def _():
                 detour(stage).wait_recv()
                 relay_aside(stage).start()
 
         def blocked(target, stage):
-            return (place == RING - 1) & (target == row * RING) & crowded(stage)
+            return (place == RING - 1) & (target == row * RING) & crowded(stage, row)
 
         others = gathered.at[pl.ds(0, GROUP - 1)]
 
@@ -548,14 +554,14 @@
             return carry
 
         with jax.named_scope("spread"):
-            @pl.when(place == RING - 1)
+            @pl.when((place == RING - 1) & crowded(0, row))
             def _():
                 detour(0).start()
 
             lax.fori_loop(1, GROUP, spread, 0)
         gathered[member] = offset[piece(member)]
         early = jnp.where(place == RING - 1, EARLY_WRAP + group * WRAP_STEP // 2, EARLY + count(place == 0) * EARLY_ZERO + group * EARLY_STEP // 2)
-        early = jnp.minimum(early, TILES)
+        early = jnp.minimum(early + LAST_WRAP * count((place == RING - 1) & (group == groups - 1)), TILES)
         early = jnp.maximum(early, first_pushes)
         lax.fori_loop(first_pushes, early, push_only, 0)
         with jax.named_scope("halo2"):
@@ -630,7 +636,7 @@
             return carry
 
         with jax.named_scope("give"):
-            @pl.when((place == RING - 1) & crowded(1))
+            @pl.when((place == RING - 1) & crowded(1, row))
             def _():
                 detour(1).start()
 
@@ -675,7 +681,7 @@
         all_of(others, scatter_send, scatter_recv).wait_send()
 
         for stage in range(2):
-            @pl.when((place == 0) & crowded(stage))
+            @pl.when((place == 0) & crowded(stage, 1 - row))
             def _():
                 relay_aside(stage).wait_send()
 
@@ -697,13 +703,15 @@
         lax.fori_loop(0, TILES, restore, 0)
 
 
-def deliver(start_ref, nodes_ref, start_hbm, nodes_hbm, sems):
-    copies = [pltpu.make_async_copy(nodes_ref.at[i], nodes_hbm.at[i], sems.at[i]) for i in range(4)]
-    copies += [pltpu.make_async_copy(start_ref.at[i], start_hbm.at[i], sems.at[4 + i]) for i in range(2)]
-    for copy in copies:
+def deliver(start_ref, nodes_ref, start_hbm, nodes_hbm, sem):
+    def copies(source, target, planes):
+        return [pltpu.make_async_copy(source.at[i, pl.ds(row, DELIVER_ROWS)], target.at[i, pl.ds(row, DELIVER_ROWS)], sem)
+                for i in range(planes) for row in range(0, ROWS, DELIVER_ROWS)]
+
+    for copy in copies(nodes_ref, nodes_hbm, 4) + copies(start_ref, start_hbm, 2):
         copy.start()
-    for copy in copies:
-        copy.wait()
+    pltpu.make_async_copy(nodes_ref, nodes_hbm, sem).wait()
+    pltpu.make_async_copy(start_ref, start_hbm, sem).wait()
 
 
 def solution(mesh):
@@ -760,7 +768,7 @@
             out_shape=(jax.ShapeDtypeStruct((2, ROWS, KY), F32), jax.ShapeDtypeStruct((4, ROWS, KY), F32)),
             in_specs=[vmem, vmem],
             out_specs=(hbm, hbm),
-            scratch_shapes=[dma((6,))],
+            scratch_shapes=[dma],
             compiler_params=pltpu.CompilerParams(vmem_limit_bytes=2**20),
             name="deliver",
         )(next_start, nodes)

time: 28.3 us -> 27.7 us (0.979)
  Pallas kernels: 27.3 us -> 26.6 us
    pallas_call x1, Pallas kernels: 25.6 us -> 25 us  [body(): pl.pallas_call(functools.partial(kernel, tm_size, space_size), out_shape=...]
where the time goes in v5:
time: 27.7 us; the launch traced here: 27.3 us
  Pallas kernels  26.6 us (96%)
  between operations  0.64 us (2%)
    pallas_call x1, Pallas kernels, body(): pl.pallas_call(functools.partial(kernel, tm_size, space_size), out_shape=...  25 us
    pallas_call x1, Pallas kernels, body(): pl.pallas_call(deliver, out_shape=(jax.ShapeDtypeStruct((2, ROWS, KY), F3...  1.65 us

profile of v5, /device:TPU:196, one launch (start us, length us, event | category | flops | bytes accessed | tf_op | source)
XLA Modules:
  0.0 27.3 jit_solution(12352567635799125065)
XLA Ops:
  0.6 25.0 %pfasst.1 = (f32[2,128,1024]{2,1,0:T(8,128)S(1)}, f32[4,128,1024]{2,1,0:T(8,128)S(1)}) custom-call(f32[2,128,1024]{2,1,0:T(8,128)} %bitcast.5, f32[4,128,1024]{2,1,0:T(8,128)} %bitcast.4), custom_call_target="tpu_custom_call" | custom-call | tf_op jit(solution)/shard_map/pfasst/pallas_call | solution.py:724
  25.6 1.6 %deliver.1 = (f32[2,128,1024]{2,1,0:T(8,128)}, f32[4,128,1024]{2,1,0:T(8,128)}) custom-call(f32[2,128,1024]{2,1,0:T(8,128)S(1)} %get-tuple-element.6.start_ref, f32[4,128,1024]{2,1,0:T(8,128)S(1)} %get-tuple-element.7.nodes_ref), custom_call_target="tpu_custom_call" | custom-call | tf_op jit(solution)/shard_map/deliver/pallas_call | solution.py:766

commit v6 on v5

--- a/solution.py
+++ b/solution.py
@@ -35,7 +35,7 @@
 LAST_WRAP = 2
 LAST_FIRST = 0
 LEAD = 1
-DELIVER_ROWS = 32
+DELIVER_ROWS = 16
 EARLY_ZERO = 2
 LAG = 6
 FIRST = 2

time: 27.7 us -> 27.7 us (level)
  no operation moved by 1% of the time
where the time goes in v6:
time: 27.7 us; the launch traced here: 27.3 us
  Pallas kernels  26.6 us (96%)
  between operations  0.64 us (2%)
    pallas_call x1, Pallas kernels, body(): pl.pallas_call(functools.partial(kernel, tm_size, space_size), out_shape=...  25 us
    pallas_call x1, Pallas kernels, body(): pl.pallas_call(deliver, out_shape=(jax.ShapeDtypeStruct((2, ROWS, KY), F3...  1.63 us

profile of v6, /device:TPU:196, one launch (start us, length us, event | category | flops | bytes accessed | tf_op | source)
XLA Modules:
  0.0 27.3 jit_solution(14084963080159704033)
XLA Ops:
  0.6 25.0 %pfasst.1 = (f32[2,128,1024]{2,1,0:T(8,128)S(1)}, f32[4,128,1024]{2,1,0:T(8,128)S(1)}) custom-call(f32[2,128,1024]{2,1,0:T(8,128)} %bitcast.5, f32[4,128,1024]{2,1,0:T(8,128)} %bitcast.4), custom_call_target="tpu_custom_call" | custom-call | tf_op jit(solution)/shard_map/pfasst/pallas_call | solution.py:724
  25.6 1.6 %deliver.1 = (f32[2,128,1024]{2,1,0:T(8,128)}, f32[4,128,1024]{2,1,0:T(8,128)}) custom-call(f32[2,128,1024]{2,1,0:T(8,128)S(1)} %get-tuple-element.6.start_ref, f32[4,128,1024]{2,1,0:T(8,128)S(1)} %get-tuple-element.7.nodes_ref), custom_call_target="tpu_custom_call" | custom-call | tf_op jit(solution)/shard_map/deliver/pallas_call | solution.py:766
